TPU v7x, 256 devices: a whole 4x4x8 slice. The times are simulated.
256 devices in a mesh: gx: 64 (over x, z_hi, y), gy: 4 (over z_lo, core).
Axes of the slice: x: 4, y: 4, z: 8 (z_hi: 4, z_lo: 2; z = z_hi * 2 + z_lo), core: 2. Of those that a mesh axis runs over, the one named last changes fastest.
Arguments:
- displacement: float32 [3, 192, 32, 128], P(None, 'gx', 'gy'), may hold values from -0.1 to 0.1
- velocity: float32 [3, 192, 32, 128], P(None, 'gx', 'gy'), may hold values from -0.6 to 0.6
- bone: int32 [192, 32, 128], P('gx', 'gy'), may hold values 0 or 1
- broken: int32 [4, 192, 32, 128], P(None, 'gx', 'gy'), may hold values from 0 to 65535, as said below
Outputs:
- velocity_end: float32 [3, 192, 32, 128], P(None, 'gx', 'gy')
- damage: float32 [192, 32, 128], P('gx', 'gy')
Inputs may be any that keep to these rules, and one draw needn't show every extreme that they name: 1 marks bone, 0 void. `broken`: only the bits that flag bonds are used: bits 0 to 15 of word 0 and bits 0 to 14 of words 1 to 3.
All inputs are finite; a program needn't handle non-finite values. No bound on the sum of `bone` on one device may be relied on, other than what follows from the above.
Results may differ from a plain program's by a relative error of at most 0.000069.
Values sent between devices are 32-bit elements; how exact they have to be, the bound alone decides.
No kernel may reach another device: no remote copies, remote signals or barrier semaphores. Data moves between devices by JAX's collectives and lax.ppermute only.
A program may use at most 128 MiB of HBM per device.

v0:
```python
import math

import jax
import jax.numpy as jnp
from jax import lax
from jax.experimental import pallas as pl
from jax.experimental.pallas import tpu as pltpu
from jax.sharding import PartitionSpec as P

BULK_TERM = -50.0
SHEAR_TERM = 1500.0
TIME_STEP = 0.1
STRETCH_CRITICAL = 0.04
STRETCH_WIDTH = 0.01
DIRECTION_EPS = 1e-06

REACH = 3
HALF = 0.5 / STRETCH_WIDTH
PEN = 0.5 * STRETCH_CRITICAL / STRETCH_WIDTH
LOST = 1024.0
F32 = jnp.float32
VMEM_LIMIT = 20 * 1024 * 1024


def half_bonds():
    listed = []
    for step_x in range(0, 4):
        for step_y in range(-3, 4):
            for step_z in range(-3, 4):
                forward_half = step_x > 0 or (
                    step_x == 0 and (step_y > 0 or (step_y == 0 and step_z > 0))
                )
                if forward_half and step_x * step_x + step_y * step_y + step_z * step_z <= 9:
                    listed.append((step_x, step_y, step_z))
    return listed


def flag_place(number):
    if number < 16:
        return (0, number)
    return (1 + (number - 16) // 15, (number - 16) % 15)


def bond_classes():
    classes = {}
    for number, (a, b, c) in enumerate(half_bonds()):
        word, bit = flag_place(number)
        group = classes.setdefault(a * a + b * b + c * c, [])
        group.append((a, b, c, word, bit, False))
        group.append((-a, -b, -c, word, bit, True))
    place = 0
    for squared in sorted(classes):
        classes[squared] = [bond + (place + k,) for k, bond in enumerate(classes[squared])]
        place += len(classes[squared])
    return {squared: classes[squared] for squared in sorted(classes)}, place


CLASSES, BONDS = bond_classes()


def pairwise(values, axis, odd):
    pairs = []
    for i in range(1 if odd else 0, lax.axis_size(axis) - 1, 2):
        pairs += [(i, i + 1), (i + 1, i)]
    return lax.ppermute(values, axis, pairs)


def both(odd_values, even_values, axis):
    return pairwise(odd_values, axis, True), pairwise(even_values, axis, False)


def call(kernel, outs, *operands, scratch=(), hbm=()):
    vmem = pl.BlockSpec(memory_space=pltpu.VMEM)
    spaces = [pltpu.HBM if n in hbm else pltpu.VMEM for n in range(len(operands))]
    held = [pltpu.with_memory_space_constraint(value, space) for value, space in zip(operands, spaces)]
    return pl.pallas_call(
        kernel,
        out_shape=outs,
        in_specs=[pl.BlockSpec(memory_space=space) for space in spaces],
        out_specs=jax.tree.map(lambda _: vmem, outs),
        scratch_shapes=list(scratch),
        compiler_params=pltpu.CompilerParams(vmem_limit_bytes=VMEM_LIMIT),
    )(*held)


def is_even(axis):
    return lax.axis_index(axis) % 2 == 0


def needed_rows(distance):
    return (6, 5, 5, 3)[distance]


def outer_rows(distance):
    return (3, 2, 2, 0)[distance]


def word_reach():
    reach = [0, 0, 0, 0]
    for number, (a, b, c) in enumerate(half_bonds()):
        word = flag_place(number)[0]
        reach[word] = max(reach[word], a)
    return reach


MOVING = [(f, x) for f in range(3) for x in range(3)]
SENT = MOVING + [(3, x) for x in range(3)]
SENT += [(4 + w, x) for w in range(4) for x in range(3 - word_reach()[w], 3)]
KEPT = [(4 + w, x) for w in range(4) for x in range(3) if (4 + w, x) not in SENT]


def strips(fields):
    placed, start = {}, 0
    for f in fields:
        for x in range(-3, 6):
            if f >= 4 and (x >= 3 or (x < 0 and (f, x + 3) not in SENT)):
                continue
            rows = needed_rows(max(0, -x, x - 2))
            placed[f, x] = (start, rows)
            start += rows
    return placed, start


ALL_STRIPS, ALL_ROWS = strips(range(8))
MOVING_STRIPS, MOVING_ROWS = strips(range(3))


def shifted(values, c):
    if c == 0:
        return values
    return pltpu.roll(values, (-c) % values.shape[-1], values.ndim - 1)


def pack_kernel(u_ref, bone_ref, broken_ref, sent_ref, kept_ref, bone_in, broken_in, sems):
    copies = [
        pltpu.make_async_copy(bone_ref, bone_in, sems.at[0]),
        pltpu.make_async_copy(broken_ref, broken_in, sems.at[1]),
    ]
    copies += [
        pltpu.make_async_copy(u_ref.at[f], sent_ref.at[3 * f : 3 * f + 3], sems.at[2 + f]) for f in range(3)
    ]
    for copy in copies:
        copy.start()
    copies[0].wait()
    sent_ref[9:12] = bone_in[...].astype(F32)
    copies[1].wait()
    for target, listed in ((sent_ref, SENT), (kept_ref, KEPT)):
        for n, (f, x) in enumerate(listed):
            if f >= 4:
                target[n] = broken_in[f - 4, x].astype(F32)
    for copy in copies[2:]:
        copy.wait()


def cut_strips(tile_of, placed, odd_ref, even_ref):
    even = is_even("gy")
    for (f, x), (start, rows) in placed.items():
        tile = tile_of(f, x)
        first, last = tile[0:rows], tile[tile.shape[0] - rows :]
        odd_ref[start : start + rows] = jnp.where(even, first, last)
        even_ref[start : start + rows] = jnp.where(even, last, first)


def widen_kernel(sent_ref, kept_ref, odd_ref, even_ref, side_ref, to_odd_ref, to_even_ref):
    even = is_even("gx")
    side_ref[0] = jnp.where(even, odd_ref[...], even_ref[...])
    side_ref[1] = jnp.where(even, even_ref[...], odd_ref[...])
    cut_strips(tiles(side_ref, sent_ref, kept_ref), ALL_STRIPS, to_odd_ref, to_even_ref)


def widen_moving_kernel(own_ref, odd_ref, even_ref, side_ref, to_odd_ref, to_even_ref):
    even = is_even("gx")
    side_ref[0] = jnp.where(even, odd_ref[...], even_ref[...])
    side_ref[1] = jnp.where(even, even_ref[...], odd_ref[...])
    cut_strips(tiles(side_ref, own_ref, None), MOVING_STRIPS, to_odd_ref, to_even_ref)


def tiles(side_ref, own_ref, kept_ref):
    def tile_of(f, x):
        if x < 0:
            return side_ref[0, SENT.index((f, x + 3))]
        if x >= 3:
            return side_ref[1, SENT.index((f, x - 3))]
        if (f, x) in KEPT:
            return kept_ref[KEPT.index((f, x))]
        return own_ref[SENT.index((f, x))]

    return tile_of


def lay(field_ref, f, tile_of, placed, odd_ref, even_ref):
    even = is_even("gy")
    rows = field_ref.shape[1] // 3
    field_ref[...] = jnp.zeros(field_ref.shape, F32)
    for x in range(-3, 6):
        if (f, x) in placed:
            start, count = placed[f, x]
            from_odd, from_even = odd_ref[start : start + count], even_ref[start : start + count]
            field_ref[x + 3, rows - count : rows] = jnp.where(even, from_odd, from_even)
            field_ref[x + 3, rows : 2 * rows] = tile_of(f, x)
            field_ref[x + 3, 2 * rows : 2 * rows + count] = jnp.where(even, from_even, from_odd)
    return field_ref[...]


def fill_moving(tile_of, placed, odd_ref, even_ref, field_ref, rolled_ref, own_ref, cells, region):
    first, last = region
    for f in range(3):
        field = lay(field_ref.at[f], f, tile_of, placed, odd_ref, even_ref)
        for c in range(-REACH, REACH + 1):
            rolled_ref[c + REACH, f] = shifted(field, c)
    for f in range(3):
        here = rolled_ref[REACH, f, cells : 2 * cells, first:last]
        for step in range(-REACH, REACH + 1):
            own_ref[f, step + REACH] = here - float(step)


def window(rolled_ref, c, f, a, b, cells, first, last):
    return rolled_ref[c + REACH, f, cells + a : 2 * cells + a, first + b : last + b]


def bond_pass(rolled_ref, own_ref, pen_of, along_ref, across_ref, cells, region, kinds):
    first, last = region
    shape = (cells, last - first, own_ref.shape[-1])
    totals = jnp.zeros(shape, F32)
    second = jnp.zeros(shape, F32)
    for squared, bonds in CLASSES.items():
        natural = math.sqrt(squared)
        moved = jnp.zeros(shape, F32)
        other = jnp.zeros(shape, F32)
        for a, b, c, word, bit, backward, place in bonds:
            rel = [
                window(rolled_ref, c, f, a, b, cells, first, last) - own_ref[f, step + REACH]
                for f, step in enumerate((a, b, c))
            ]
            square = rel[0] * rel[0] + rel[1] * rel[1] + rel[2] * rel[2]
            length = square * lax.rsqrt(jnp.maximum(square, 1e-30))
            scaled = (length - natural) * (HALF / natural)
            pen = pen_of(a, b, c, word, bit, backward, place)
            weight = 1.0 + jnp.tanh(pen - scaled)
            pulled = weight * scaled
            direction = lax.rsqrt(square + DIRECTION_EPS)
            along_ref[place] = weight * direction
            across_ref[place] = pulled * direction
            moved = moved + pulled
            other = other + (pen if kinds == "volume" else weight)
        totals = totals + moved * (0.5 * natural / HALF)
        if kinds == "volume":
            lost = (PEN * len(bonds) - other) * (1.0 / LOST)
            second = second + (len(bonds) - lost) * natural
        else:
            second = second + other * (0.5 * natural)
    return totals, second


def cut_ratio(ratio_ref, to_odd_ref, to_even_ref, rows):
    even = is_even("gx")
    half = rows // 2
    start = 0
    for f in range(ratio_ref.shape[0]):
        for distance in range(1, 4):
            count = rows + 2 * outer_rows(distance)
            part = slice(half - outer_rows(distance), half + rows + outer_rows(distance))
            upper = ratio_ref[f, 3 - distance, part]
            lower = ratio_ref[f, distance - 1, part]
            to_odd_ref[start : start + count] = jnp.where(even, lower, upper)
            to_even_ref[start : start + count] = jnp.where(even, upper, lower)
            start += count


def ratio_rows(rows):
    return sum(rows + 2 * outer_rows(distance) for distance in range(1, 4))


def first_kernel(side_ref, sent_ref, kept_ref, odd_ref, even_ref, v_hbm, rolled_ref, pen_ref, along_ref, across_ref, ratio_ref, to_odd_ref, to_even_ref, volume_ref, v_ref, mine_ref, field_ref, nb_ref, word_ref, sem):
    copy = pltpu.make_async_copy(v_hbm, v_ref, sem)
    copy.start()
    rows = sent_ref.shape[-2]
    depth = sent_ref.shape[-1]
    cells = pen_ref.shape[1]
    half = rows // 2
    region = (half, half + 2 * rows)
    tile_of = tiles(side_ref, sent_ref, kept_ref)
    fill_moving(tile_of, ALL_STRIPS, odd_ref, even_ref, field_ref, rolled_ref, mine_ref, cells, region)
    bone = lay(field_ref.at[0], 3, tile_of, ALL_STRIPS, odd_ref, even_ref)
    void = jnp.where(bone == 0.0, -1, 0)
    lane = lax.broadcasted_iota(jnp.int32, void.shape, 2)
    for c in range(-REACH, REACH + 1):
        turned = shifted(void, c)
        if c != 0:
            turned = jnp.where((lane + c >= 0) & (lane + c < depth), turned, -1)
        nb_ref[c + REACH] = turned
    for w in range(4):
        words = lay(field_ref.at[1 + w % 2], 4 + w, tile_of, ALL_STRIPS, odd_ref, even_ref)
        words = words[0 : 2 * cells].astype(jnp.int32)
        for c in range(-REACH, REACH + 1):
            word_ref[c + REACH, w] = shifted(words, c) | nb_ref[c + REACH, 0 : 2 * cells]

    first, last = region

    def pen_of(a, b, c, word, bit, backward, place):
        if backward:
            words = word_ref[c + REACH, word, cells + a : 2 * cells + a, first + b : last + b]
            hit = words & (1 << bit)
        else:
            words = word_ref[REACH, word, cells : 2 * cells, first:last]
            far = nb_ref[c + REACH, cells + a : 2 * cells + a, first + b : last + b]
            hit = (words & (1 << bit)) | far
        pen = jnp.where(hit == 0, PEN, PEN - LOST)
        pen_ref[place] = pen
        return pen

    totals, volume = bond_pass(rolled_ref, mine_ref, pen_of, along_ref, across_ref, cells, region, "volume")
    solid = jnp.where(nb_ref[REACH, cells : 2 * cells, first:last] == 0, 1.0, 0.0)
    volume = jnp.maximum(volume * solid, 1.0)
    inverse = 1.0 / volume
    dilatation = 3.0 * (totals * solid) / volume
    ratio_ref[0] = dilatation * inverse * (0.5 * BULK_TERM)
    ratio_ref[1] = inverse * (0.5 * SHEAR_TERM / HALF)
    cut_ratio(ratio_ref, to_odd_ref, to_even_ref, rows)
    volume_ref[0] = volume
    volume_ref[1] = solid
    copy.wait()


def later_kernel(side_ref, own_ref, odd_ref, even_ref, pen_ref, volume_ref, rolled_ref, along_ref, across_ref, ratio_ref, to_odd_ref, to_even_ref, damage_ref, mine_ref, field_ref):
    rows = own_ref.shape[-2]
    cells = pen_ref.shape[1]
    half = rows // 2
    region = (half, half + 2 * rows)
    tile_of = tiles(side_ref, own_ref, None)
    fill_moving(tile_of, MOVING_STRIPS, odd_ref, even_ref, field_ref, rolled_ref, mine_ref, cells, region)

    def pen_of(a, b, c, word, bit, backward, place):
        return pen_ref[place]

    totals, held = bond_pass(rolled_ref, mine_ref, pen_of, along_ref, across_ref, cells, region, "weight")
    volume = volume_ref[0]
    solid = volume_ref[1]
    inverse = 1.0 / volume
    dilatation = 3.0 * (totals * solid) / volume
    ratio_ref[0] = dilatation * inverse * (0.5 * BULK_TERM)
    cut_ratio(ratio_ref, to_odd_ref, to_even_ref, rows)
    damage = 1.0 - (held * solid) / volume
    damage_ref[...] = damage[:, half : half + rows]


def forces(total, inner, rolled_ref, along_ref, across_ref, scaled_ref, inverse_ref, rows):
    half = rows // 2
    mine = slice(half, half + rows)
    for x in range(3):
        scaled = scaled_ref[REACH, x + 3, mine]
        inverse = inverse_ref[REACH, x + 3, mine]
        here = [rolled_ref[REACH, f, x + 3, rows : 2 * rows] for f in range(3)]
        for bonds in CLASSES.values():
            for a, b, c, word, bit, backward, place in bonds:
                if (0 <= x + a < 3) != inner:
                    continue
                far = (c + REACH, x + 3 + a, slice(half + b, half + rows + b))
                magnitude = along_ref[place, x, mine] * (scaled + scaled_ref[far])
                magnitude = magnitude + across_ref[place, x, mine] * (inverse + inverse_ref[far])
                for f, step in enumerate((a, b, c)):
                    rel = rolled_ref[c + REACH, f, x + 3 + a, rows + b : 2 * rows + b] - here[f]
                    if step:
                        rel = rel + float(step)
                    total[f][x] = total[f][x] + magnitude * rel
    return total


def fill_inner(target_ref, own):
    for c in range(-REACH, REACH + 1):
        target_ref[c + REACH, 3:6] = shifted(own, c)


def fill_outer(target_ref, field_ref, f, odd_ref, even_ref, rows):
    even = is_even("gx")
    half = rows // 2
    field_ref[...] = jnp.zeros(field_ref.shape, F32)
    start = f * ratio_rows(rows)
    for distance in range(1, 4):
        count = rows + 2 * outer_rows(distance)
        part = slice(half - outer_rows(distance), half + rows + outer_rows(distance))
        from_odd, from_even = odd_ref[start : start + count], even_ref[start : start + count]
        field_ref[3 - distance, part] = jnp.where(even, from_odd, from_even)
        field_ref[2 + distance, part] = jnp.where(even, from_even, from_odd)
        start += count
    field = field_ref[...]
    for c in range(-REACH, REACH + 1):
        turned = shifted(field, c)
        target_ref[c + REACH, 0:3] = turned[0:3]
        target_ref[c + REACH, 6:9] = turned[3:6]


def start_total(rows, depth):
    return [[jnp.zeros((rows, depth), F32) for _ in range(3)] for _ in range(3)]


def inner_kernel(rolled_ref, along_ref, across_ref, ratio_ref, held_ref, part_ref, scaled_ref, inverse_ref):
    rows, depth = part_ref.shape[2:]
    fill_inner(scaled_ref, ratio_ref[0])
    if held_ref is None:
        held_ref = inverse_ref
        fill_inner(inverse_ref, ratio_ref[1])
    total = forces(start_total(rows, depth), True, rolled_ref, along_ref, across_ref, scaled_ref, held_ref, rows)
    for f in range(3):
        for x in range(3):
            part_ref[f, x] = total[f][x]


def first_inner_kernel(rolled_ref, along_ref, across_ref, ratio_ref, part_ref, scaled_ref, inverse_ref):
    inner_kernel(rolled_ref, along_ref, across_ref, ratio_ref, None, part_ref, scaled_ref, inverse_ref)


def last_inner_kernel(rolled_ref, along_ref, across_ref, ratio_ref, inverse_ref, part_ref, scaled_ref):
    inner_kernel(rolled_ref, along_ref, across_ref, ratio_ref, inverse_ref, part_ref, scaled_ref, None)


def outer_forces(rolled_ref, along_ref, across_ref, scaled_ref, inverse_ref, part_ref, rows):
    total = [[part_ref[f, x] for x in range(3)] for f in range(3)]
    return forces(total, False, rolled_ref, along_ref, across_ref, scaled_ref, inverse_ref, rows)


def move_kernel(rolled_ref, along_ref, across_ref, ratio_ref, part_ref, odd_ref, even_ref, volume_ref, sent_ref, v_ref, u_out, v_out, inverse_ref, scaled_ref, field_ref):
    rows = v_ref.shape[2]
    half = rows // 2
    for f, target in ((0, scaled_ref), (1, inverse_ref)):
        fill_outer(target, field_ref.at[f], f, odd_ref, even_ref, rows)
        fill_inner(target, ratio_ref[f])
    total = outer_forces(rolled_ref, along_ref, across_ref, scaled_ref, inverse_ref, part_ref, rows)
    for f in range(3):
        for x in range(3):
            speed = v_ref[f, x] + TIME_STEP * (total[f][x] * volume_ref[1, x, half : half + rows])
            v_out[f, x] = speed
            u_out[3 * f + x] = sent_ref[3 * f + x] + TIME_STEP * speed


def last_kernel(rolled_ref, along_ref, across_ref, ratio_ref, part_ref, odd_ref, even_ref, volume_ref, v_ref, inverse_ref, damage_ref, v_out, damage_out, scaled_ref, field_ref):
    rows = v_ref.shape[2]
    half = rows // 2
    damage_out[...] = damage_ref[...]
    fill_outer(scaled_ref, field_ref, 0, odd_ref, even_ref, rows)
    scaled_ref[REACH, 3:6] = ratio_ref[0]
    total = outer_forces(rolled_ref, along_ref, across_ref, scaled_ref, inverse_ref, part_ref, rows)
    for f in range(3):
        for x in range(3):
            v_out[f, x] = v_ref[f, x] + TIME_STEP * (total[f][x] * volume_ref[1, x, half : half + rows])


def body(displacement, velocity, bone, broken):
    cells, rows, depth = bone.shape
    if cells != REACH or rows != 8:
        raise ValueError("block size")
    layers, tall, region = 3 * cells, 3 * rows, 2 * rows
    turns = 2 * REACH + 1

    def vmem(*shape, dtype=F32):
        return pltpu.VMEM(shape, dtype)

    hbm = jax.ShapeDtypeStruct
    sent, kept = call(
        pack_kernel,
        (vmem(len(SENT), rows, depth), vmem(len(KEPT), rows, depth)),
        displacement,
        bone,
        broken,
        scratch=(
            vmem(cells, rows, depth, dtype=jnp.int32),
            vmem(4, cells, rows, depth, dtype=jnp.int32),
            pltpu.SemaphoreType.DMA((5,)),
        ),
        hbm=(0, 1, 2),
    )
    side, to_odd, to_even = call(
        widen_kernel,
        (vmem(2, len(SENT), rows, depth), vmem(ALL_ROWS, depth), vmem(ALL_ROWS, depth)),
        sent,
        kept,
        *both(sent, sent, "gx"),
    )
    bonds = (BONDS, cells, region, depth)
    crossing = ratio_rows(rows)
    rolled, pen, along, across, ratio, to_odd, to_even, volume, speed = call(
        first_kernel,
        (
            vmem(turns, 3, layers, tall, depth),
            vmem(*bonds),
            vmem(*bonds),
            vmem(*bonds),
            vmem(2, cells, region, depth),
            vmem(2 * crossing, depth),
            vmem(2 * crossing, depth),
            vmem(2, cells, region, depth),
            vmem(3, cells, rows, depth),
        ),
        side,
        sent,
        kept,
        *both(to_odd, to_even, "gy"),
        velocity,
        scratch=(
            vmem(3, turns, cells, region, depth),
            vmem(3, layers, tall, depth),
            vmem(turns, layers, tall, depth, dtype=jnp.int32),
            vmem(turns, 4, 2 * cells, tall, depth, dtype=jnp.int32),
            pltpu.SemaphoreType.DMA(()),
        ),
        hbm=(5,),
    )
    arrived = both(to_odd, to_even, "gx")
    wide_ratio = vmem(turns, layers, region, depth)
    part = call(
        first_inner_kernel, vmem(3, cells, rows, depth), rolled, along, across, ratio, scratch=(wide_ratio, wide_ratio)
    )
    moved, speed, inverse = call(
        move_kernel,
        (vmem(3 * cells, rows, depth), vmem(3, cells, rows, depth), wide_ratio),
        rolled,
        along,
        across,
        ratio,
        part,
        *arrived,
        volume,
        sent,
        speed,
        scratch=(wide_ratio, vmem(2, 6, region, depth)),
    )
    side, to_odd, to_even = call(
        widen_moving_kernel,
        (vmem(2, len(MOVING), rows, depth), vmem(MOVING_ROWS, depth), vmem(MOVING_ROWS, depth)),
        moved,
        *both(moved, moved, "gx"),
    )
    rolled, along, across, ratio, to_odd, to_even, damage = call(
        later_kernel,
        (
            vmem(turns, 3, layers, tall, depth),
            vmem(*bonds),
            vmem(*bonds),
            vmem(1, cells, region, depth),
            vmem(crossing, depth),
            vmem(crossing, depth),
            vmem(cells, rows, depth),
        ),
        side,
        moved,
        *both(to_odd, to_even, "gy"),
        pen,
        volume,
        scratch=(
            vmem(3, turns, cells, region, depth),
            vmem(3, layers, tall, depth),
        ),
    )
    arrived = both(to_odd, to_even, "gx")
    part = call(
        last_inner_kernel, vmem(3, cells, rows, depth), rolled, along, across, ratio, inverse, scratch=(wide_ratio,)
    )
    return call(
        last_kernel,
        (hbm((3, cells, rows, depth), F32), hbm((cells, rows, depth), F32)),
        rolled,
        along,
        across,
        ratio,
        part,
        *arrived,
        volume,
        speed,
        inverse,
        damage,
        scratch=(wide_ratio, vmem(6, region, depth)),
    )


def solution(mesh):
    in_specs = (
        P(None, "gx", "gy", None),
        P(None, "gx", "gy", None),
        P("gx", "gy", None),
        P(None, "gx", "gy", None),
    )
    out_specs = (P(None, "gx", "gy", None), P("gx", "gy", None))
    return jax.shard_map(body, mesh=mesh, in_specs=in_specs, out_specs=out_specs, check_vma=False)
```

profile of v0, /device:TPU:38, one launch (start us, length us, event | category | flops | bytes accessed | tf_op | source)
XLA Modules:
  0.0 70.3 jit_solution(14709310678289848909)
XLA Ops:
  0.6 0.9 %shard_map.59 = (f32[19,8,128]{2,1,0:T(8,128)S(1)}, f32[5,8,128]{2,1,0:T(8,128)S(1)}) custom-call(f32[3,3,8,128]{3,2,1,0:T(8,128)} %u_ref.1, s32[3,8,128]{2,1,0:T(8,128)} %bone_ref.1, s32[4,3,8,128]{3,2,1,0:T(8,128)} %broken_ref.1), custom_call_target="tpu_custom_call" | custom-call | tf_op jit(solution)/shard_map/pallas_call | solution.py:76
  1.5 1.7 %collective-permute-start.1 = (f32[19,8,128]{2,1,0:T(8,128)S(1)}, f32[19,8,128]{2,1,0:T(8,128)S(1)}, u32[]{:S(2)}, u32[]{:S(2)}) collective-permute-start(f32[19,8,128]{2,1,0:T(8,128)S(1)} %get-tuple-element.29.sent_ref), channel_id=1, source_target_pairs={{0,4},{4,0},{8,12},{12,8},{16,20},{20,16},{24,28},{28,24},{32,36},... | collective-permute-start | bytes 233480 | tf_op jit(solution)/shard_map/ppermute | solution.py:65
  3.2 9.2 %collective-permute-start = (f32[19,8,128]{2,1,0:T(8,128)S(1)}, f32[19,8,128]{2,1,0:T(8,128)S(1)}, u32[]{:S(2)}, u32[]{:S(2)}) collective-permute-start(f32[19,8,128]{2,1,0:T(8,128)S(1)} %get-tuple-element.29.sent_ref), channel_id=1, source_target_pairs={{4,8},{8,4},{12,16},{16,12},{20,24},{24,20},{28,32},{32,28},{36,40... | collective-permute-start | bytes 233480 | tf_op jit(solution)/shard_map/ppermute | solution.py:65
  12.4 3.7 %collective-permute-done.odd_ref = f32[19,8,128]{2,1,0:T(8,128)S(1)} collective-permute-done((f32[19,8,128]{2,1,0:T(8,128)S(1)}, f32[19,8,128]{2,1,0:T(8,128)S(1)}, u32[]{:S(2)}, u32[]{:S(2)}) %collective-permute-start) | collective-permute-done | bytes 77856 | tf_op jit(solution)/shard_map/ppermute | solution.py:65
  16.1 1.9 %collective-permute-start.2 = (f32[281,128]{1,0:T(8,128)S(1)}, f32[281,128]{1,0:T(8,128)S(1)}, u32[]{:S(2)}, u32[]{:S(2)}) collective-permute-start(f32[281,128]{1,0:T(8,128)S(1)} %get-tuple-element.32), channel_id=1, source_target_pairs={{1,2},{2,1},{5,6},{6,5},{9,10},{10,9},{13,14},{14,13},{17,18},{18,... | collective-permute-start | bytes 431624 | tf_op jit(solution)/shard_map/ppermute | solution.py:65
  18.1 0.1 collective-permute-start.3
  18.2 4.4 %collective-permute-done.2.odd_ref = f32[281,128]{1,0:T(8,128)S(1)} collective-permute-done((f32[281,128]{1,0:T(8,128)S(1)}, f32[281,128]{1,0:T(8,128)S(1)}, u32[]{:S(2)}, u32[]{:S(2)}) %collective-permute-start.2) | collective-permute-done | bytes 143904 | tf_op jit(solution)/shard_map/ppermute | solution.py:65
  22.6 3.9 %shard_map.61 = (f32[7,3,9,24,128]{4,3,2,1,0:T(8,128)S(1)}, f32[122,3,16,128]{3,2,1,0:T(8,128)S(1)}, f32[122,3,16,128]{3,2,1,0:T(8,128)S(1)}, f32[122,3,16,128]{...) custom-call(f32[2,19,8,128]{3,2,1,0:T(8,128)S(1)} %get-tuple-element, ...), custom_call_target="tpu_custom_call" | custom-call | tf_op jit(solution)/shard_map/pallas_call | solution.py:76
  26.5 7.7 %collective-permute-start.4 = (f32[64,128]{1,0:T(8,128)S(1)}, f32[64,128]{1,0:T(8,128)S(1)}, u32[]{:S(2)}, u32[]{:S(2)}) collective-permute-start(f32[64,128]{1,0:T(8,128)S(1)} %get-tuple-element.38), channel_id=1, source_target_pairs={{4,8},{8,4},{12,16},{16,12},{20,24},{24,20},{28,32},{32,28},{36,40... | collective-permute-start | bytes 98312 | tf_op jit(solution)/shard_map/ppermute | solution.py:65
  34.3 0.7 %shard_map.62.part_ref = f32[3,3,8,128]{3,2,1,0:T(8,128)S(1)} custom-call(f32[7,3,9,24,128]{4,3,2,1,0:T(8,128)S(1)} %get-tuple-element.34.rolled_ref, f32[122,3,16,128]{3,2,1,0:T(8,128)S(1)} %get-tuple-element.35.along_ref, f32[122,3,16,128]{3,2,1,0:T(8,128)S(1)} %get-tuple-element.36.across_ref, f32[2,3,16,128]{3,2,1,0:T(8,128)S(1)} %get-tuple-element.37.ratio_ref), custom_call_target="tpu_custom_call" | custom-call | tf_op jit(solution)/shard_map/pallas_call | solution.py:76
  35.0 2.4 %collective-permute-done.4.odd_ref = f32[64,128]{1,0:T(8,128)S(1)} collective-permute-done((f32[64,128]{1,0:T(8,128)S(1)}, f32[64,128]{1,0:T(8,128)S(1)}, u32[]{:S(2)}, u32[]{:S(2)}) %collective-permute-start.4) | collective-permute-done | bytes 32800 | tf_op jit(solution)/shard_map/ppermute | solution.py:65
  37.4 0.8 %collective-permute-done.5.even_ref = f32[64,128]{1,0:T(8,128)S(1)} collective-permute-done((f32[64,128]{1,0:T(8,128)S(1)}, f32[64,128]{1,0:T(8,128)S(1)}, u32[]{:S(2)}, u32[]{:S(2)}) %collective-permute-start.5) | collective-permute-done | bytes 32800 | tf_op jit(solution)/shard_map/ppermute | solution.py:65
  38.2 0.6 shard_map.63
  38.8 0.1 collective-permute-start.7
  38.9 6.9 %collective-permute-start.6 = (f32[9,8,128]{2,1,0:T(8,128)S(1)}, f32[9,8,128]{2,1,0:T(8,128)S(1)}, u32[]{:S(2)}, u32[]{:S(2)}) collective-permute-start(f32[9,8,128]{2,1,0:T(8,128)S(1)} %get-tuple-element.42.own_ref), channel_id=1, source_target_pairs={{4,8},{8,4},{12,16},{16,12},{20,24},{24,20},{28,32},{32,28},{36,40... | collective-permute-start | bytes 110600 | tf_op jit(solution)/shard_map/ppermute | solution.py:65
  45.8 4.1 %collective-permute-done.6.odd_ref = f32[9,8,128]{2,1,0:T(8,128)S(1)} collective-permute-done((f32[9,8,128]{2,1,0:T(8,128)S(1)}, f32[9,8,128]{2,1,0:T(8,128)S(1)}, u32[]{:S(2)}, u32[]{:S(2)}) %collective-permute-start.6) | collective-permute-done | bytes 36896 | tf_op jit(solution)/shard_map/ppermute | solution.py:65
  49.9 1.9 %collective-permute-start.8 = (f32[132,128]{1,0:T(8,128)S(1)}, f32[132,128]{1,0:T(8,128)S(1)}, u32[]{:S(2)}, u32[]{:S(2)}) collective-permute-start(f32[132,128]{1,0:T(8,128)S(1)} %get-tuple-element.44), channel_id=1, source_target_pairs={{1,2},{2,1},{5,6},{6,5},{9,10},{10,9},{13,14},{14,13},{17,18},{18,... | collective-permute-start | bytes 202760 | tf_op jit(solution)/shard_map/ppermute | solution.py:65
  51.9 0.1 collective-permute-start.9
  52.0 3.6 %collective-permute-done.8.odd_ref = f32[132,128]{1,0:T(8,128)S(1)} collective-permute-done((f32[132,128]{1,0:T(8,128)S(1)}, f32[132,128]{1,0:T(8,128)S(1)}, u32[]{:S(2)}, u32[]{:S(2)}) %collective-permute-start.8) | collective-permute-done | bytes 67616 | tf_op jit(solution)/shard_map/ppermute | solution.py:65
  55.6 2.9 %shard_map.65 = (f32[7,3,9,24,128]{4,3,2,1,0:T(8,128)S(1)}, f32[122,3,16,128]{3,2,1,0:T(8,128)S(1)}, f32[122,3,16,128]{3,2,1,0:T(8,128)S(1)}, f32[1,3,16,128]{3,...) custom-call(f32[2,9,8,128]{3,2,1,0:T(8,128)S(1)} %get-tuple-element.43.side_ref, ...), custom_call_target="tpu_custom_call" | custom-call | tf_op jit(solution)/shard_map/pallas_call | solution.py:76
  58.5 6.9 %collective-permute-start.10 = (f32[32,128]{1,0:T(8,128)S(1)}, f32[32,128]{1,0:T(8,128)S(1)}, u32[]{:S(2)}, u32[]{:S(2)}) collective-permute-start(f32[32,128]{1,0:T(8,128)S(1)} %get-tuple-element.52), channel_id=1, source_target_pairs={{4,8},{8,4},{12,16},{16,12},{20,24},{24,20},{28,32},{32,28},{36,40... | collective-permute-start | bytes 49160 | tf_op jit(solution)/shard_map/ppermute | solution.py:65
  65.5 0.7 shard_map.66.part_ref
  66.1 3.1 %collective-permute-done.10.odd_ref = f32[32,128]{1,0:T(8,128)S(1)} collective-permute-done((f32[32,128]{1,0:T(8,128)S(1)}, f32[32,128]{1,0:T(8,128)S(1)}, u32[]{:S(2)}, u32[]{:S(2)}) %collective-permute-start.10) | collective-permute-done | bytes 16416 | tf_op jit(solution)/shard_map/ppermute | solution.py:65
  69.2 1.1 %shard_map.67 = (f32[3,3,8,128]{3,2,1,0:T(8,128)}, f32[3,8,128]{2,1,0:T(8,128)}) custom-call(f32[7,3,9,24,128]{4,3,2,1,0:T(8,128)S(1)} %get-tuple-element.47.rolled_ref, f32[122,3,16,128]{3,2,1,0:T(8,128)S(1)} %get-tuple-element.48.along_ref, f32[122,3,16,128]{3,2,1,0:T(8,128)S(1)} %get-tuple-element.49.across_ref, ...), custom_call_target="tpu_custom_call" | custom-call | tf_op jit(solution)/shard_map/pallas_call | solution.py:76
  (9 shorter events, 0.3 us)
Async XLA Ops:
  1.5 10.9 %collective-permute-start.1 = (f32[19,8,128]{2,1,0:T(8,128)S(1)}, f32[19,8,128]{2,1,0:T(8,128)S(1)}, u32[]{:S(2)}, u32[]{:S(2)}) collective-permute-start(f32[19,8,128]{2,1,0:T(8,128)S(1)} %get-tuple-element.29.sent_ref), channel_id=1, source_target_pairs={{0,4},{4,0},{8,12},{12,8},{16,20},{20,16},{24,28},{28,24},{32,36},... | collective-permute-start | bytes 233480 | tf_op jit(solution)/shard_map/ppermute | solution.py:65
  3.2 12.9 %collective-permute-start = (f32[19,8,128]{2,1,0:T(8,128)S(1)}, f32[19,8,128]{2,1,0:T(8,128)S(1)}, u32[]{:S(2)}, u32[]{:S(2)}) collective-permute-start(f32[19,8,128]{2,1,0:T(8,128)S(1)} %get-tuple-element.29.sent_ref), channel_id=1, source_target_pairs={{4,8},{8,4},{12,16},{16,12},{20,24},{24,20},{28,32},{32,28},{36,40... | collective-permute-start | bytes 233480 | tf_op jit(solution)/shard_map/ppermute | solution.py:65
  16.1 6.5 %collective-permute-start.2 = (f32[281,128]{1,0:T(8,128)S(1)}, f32[281,128]{1,0:T(8,128)S(1)}, u32[]{:S(2)}, u32[]{:S(2)}) collective-permute-start(f32[281,128]{1,0:T(8,128)S(1)} %get-tuple-element.32), channel_id=1, source_target_pairs={{1,2},{2,1},{5,6},{6,5},{9,10},{10,9},{13,14},{14,13},{17,18},{18,... | collective-permute-start | bytes 431624 | tf_op jit(solution)/shard_map/ppermute | solution.py:65
  18.1 4.5 %collective-permute-start.3 = (f32[281,128]{1,0:T(8,128)S(1)}, f32[281,128]{1,0:T(8,128)S(1)}, u32[]{:S(2)}, u32[]{:S(2)}) collective-permute-start(f32[281,128]{1,0:T(8,128)S(1)} %get-tuple-element.33), channel_id=1, source_target_pairs={{0,1},{1,0},{2,3},{3,2},{4,5},{5,4},{6,7},{7,6},{8,9},{9,8},{10,11... | collective-permute-start | bytes 431624 | tf_op jit(solution)/shard_map/ppermute | solution.py:65
  26.5 10.9 %collective-permute-start.4 = (f32[64,128]{1,0:T(8,128)S(1)}, f32[64,128]{1,0:T(8,128)S(1)}, u32[]{:S(2)}, u32[]{:S(2)}) collective-permute-start(f32[64,128]{1,0:T(8,128)S(1)} %get-tuple-element.38), channel_id=1, source_target_pairs={{4,8},{8,4},{12,16},{16,12},{20,24},{24,20},{28,32},{32,28},{36,40... | collective-permute-start | bytes 98312 | tf_op jit(solution)/shard_map/ppermute | solution.py:65
  34.2 4.0 %collective-permute-start.5 = (f32[64,128]{1,0:T(8,128)S(1)}, f32[64,128]{1,0:T(8,128)S(1)}, u32[]{:S(2)}, u32[]{:S(2)}) collective-permute-start(f32[64,128]{1,0:T(8,128)S(1)} %get-tuple-element.39), channel_id=1, source_target_pairs={{0,4},{4,0},{8,12},{12,8},{16,20},{20,16},{24,28},{28,24},{32,36},... | collective-permute-start | bytes 98312 | tf_op jit(solution)/shard_map/ppermute | solution.py:65
  38.8 7.0 %collective-permute-start.7 = (f32[9,8,128]{2,1,0:T(8,128)S(1)}, f32[9,8,128]{2,1,0:T(8,128)S(1)}, u32[]{:S(2)}, u32[]{:S(2)}) collective-permute-start(f32[9,8,128]{2,1,0:T(8,128)S(1)} %get-tuple-element.42.own_ref), channel_id=1, source_target_pairs={{0,4},{4,0},{8,12},{12,8},{16,20},{20,16},{24,28},{28,24},{32,36},... | collective-permute-start | bytes 110600 | tf_op jit(solution)/shard_map/ppermute | solution.py:65
  38.9 11.0 %collective-permute-start.6 = (f32[9,8,128]{2,1,0:T(8,128)S(1)}, f32[9,8,128]{2,1,0:T(8,128)S(1)}, u32[]{:S(2)}, u32[]{:S(2)}) collective-permute-start(f32[9,8,128]{2,1,0:T(8,128)S(1)} %get-tuple-element.42.own_ref), channel_id=1, source_target_pairs={{4,8},{8,4},{12,16},{16,12},{20,24},{24,20},{28,32},{32,28},{36,40... | collective-permute-start | bytes 110600 | tf_op jit(solution)/shard_map/ppermute | solution.py:65
  49.9 5.6 %collective-permute-start.8 = (f32[132,128]{1,0:T(8,128)S(1)}, f32[132,128]{1,0:T(8,128)S(1)}, u32[]{:S(2)}, u32[]{:S(2)}) collective-permute-start(f32[132,128]{1,0:T(8,128)S(1)} %get-tuple-element.44), channel_id=1, source_target_pairs={{1,2},{2,1},{5,6},{6,5},{9,10},{10,9},{13,14},{14,13},{17,18},{18,... | collective-permute-start | bytes 202760 | tf_op jit(solution)/shard_map/ppermute | solution.py:65
  51.9 3.7 %collective-permute-start.9 = (f32[132,128]{1,0:T(8,128)S(1)}, f32[132,128]{1,0:T(8,128)S(1)}, u32[]{:S(2)}, u32[]{:S(2)}) collective-permute-start(f32[132,128]{1,0:T(8,128)S(1)} %get-tuple-element.45), channel_id=1, source_target_pairs={{0,1},{1,0},{2,3},{3,2},{4,5},{5,4},{6,7},{7,6},{8,9},{9,8},{10,11... | collective-permute-start | bytes 202760 | tf_op jit(solution)/shard_map/ppermute | solution.py:65
  58.5 10.7 %collective-permute-start.10 = (f32[32,128]{1,0:T(8,128)S(1)}, f32[32,128]{1,0:T(8,128)S(1)}, u32[]{:S(2)}, u32[]{:S(2)}) collective-permute-start(f32[32,128]{1,0:T(8,128)S(1)} %get-tuple-element.52), channel_id=1, source_target_pairs={{4,8},{8,4},{12,16},{16,12},{20,24},{24,20},{28,32},{32,28},{36,40... | collective-permute-start | bytes 49160 | tf_op jit(solution)/shard_map/ppermute | solution.py:65
  65.4 3.9 %collective-permute-start.11 = (f32[32,128]{1,0:T(8,128)S(1)}, f32[32,128]{1,0:T(8,128)S(1)}, u32[]{:S(2)}, u32[]{:S(2)}) collective-permute-start(f32[32,128]{1,0:T(8,128)S(1)} %get-tuple-element.53), channel_id=1, source_target_pairs={{0,4},{4,0},{8,12},{12,8},{16,20},{20,16},{24,28},{28,24},{32,36},... | collective-permute-start | bytes 49160 | tf_op jit(solution)/shard_map/ppermute | solution.py:65
where the time goes:
time: 70.7 us; the launch traced here: 70.3 us
  starting transfers between devices  36.6 us (52%)
  waiting for transfers between devices  22.1 us (31%)
  Pallas kernels  10.8 us (15%)
  between operations  0.78 us (1%)
    ppermute x12, starting transfers between devices, pairwise(): return lax.ppermute(values, axis, pairs)  36.6 us
    ppermute x12, waiting for transfers between devices, pairwise(): return lax.ppermute(values, axis, pairs)  22.1 us
    pallas_call x9, Pallas kernels, call(): pl.pallas_call(kernel, out_shape=outs, in_specs=[pl.BlockSpec(memory_spac...  10.8 us
  transfers between devices with their start and end apart: 12, of which 7 were waited for; matrix products, arithmetic and copies ran while one was open for 0% of the time, Pallas kernels for 2%

commit v1 on v0

--- a/solution.py
+++ b/solution.py
@@ -56,6 +56,17 @@
 
 
 CLASSES, BONDS = bond_classes()
+DIRECTED = [bond for bonds in CLASSES.values() for bond in bonds]
+
+
+def layers_read(c, word=None):
+    reach = [
+        a for a, b, step, held, bit, backward, place in DIRECTED
+        if step == c and (word is None or (backward and held == word))
+    ]
+    if c == 0:
+        reach.append(0)
+    return slice(3 + min(reach), 6 + max(reach)) if reach else None
 
 
 def pairwise(values, axis, odd):
@@ -191,9 +202,10 @@
 def lay(field_ref, f, tile_of, placed, odd_ref, even_ref):
     even = is_even("gy")
     rows = field_ref.shape[1] // 3
-    field_ref[...] = jnp.zeros(field_ref.shape, F32)
     for x in range(-3, 6):
         if (f, x) in placed:
+            field_ref[x + 3, 0:rows] = jnp.zeros((rows, field_ref.shape[2]), F32)
+            field_ref[x + 3, 2 * rows : 3 * rows] = jnp.zeros((rows, field_ref.shape[2]), F32)
             start, count = placed[f, x]
             from_odd, from_even = odd_ref[start : start + count], even_ref[start : start + count]
             field_ref[x + 3, rows - count : rows] = jnp.where(even, from_odd, from_even)
@@ -207,49 +219,53 @@
     for f in range(3):
         field = lay(field_ref.at[f], f, tile_of, placed, odd_ref, even_ref)
         for c in range(-REACH, REACH + 1):
-            rolled_ref[c + REACH, f] = shifted(field, c)
+            part = layers_read(c)
+            rolled_ref[c + REACH, f, part] = shifted(field[part], c)
     for f in range(3):
         here = rolled_ref[REACH, f, cells : 2 * cells, first:last]
         for step in range(-REACH, REACH + 1):
             own_ref[f, step + REACH] = here - float(step)
 
 
-def window(rolled_ref, c, f, a, b, cells, first, last):
-    return rolled_ref[c + REACH, f, cells + a : 2 * cells + a, first + b : last + b]
-
-
-def bond_pass(rolled_ref, own_ref, pen_of, along_ref, across_ref, cells, region, kinds):
+def bond_pass(rolled_ref, own_ref, pen_of, square_ref, along_ref, across_ref, out_ref, region, kinds):
     first, last = region
-    shape = (cells, last - first, own_ref.shape[-1])
-    totals = jnp.zeros(shape, F32)
-    second = jnp.zeros(shape, F32)
-    for squared, bonds in CLASSES.items():
-        natural = math.sqrt(squared)
-        moved = jnp.zeros(shape, F32)
-        other = jnp.zeros(shape, F32)
-        for a, b, c, word, bit, backward, place in bonds:
-            rel = [
-                window(rolled_ref, c, f, a, b, cells, first, last) - own_ref[f, step + REACH]
-                for f, step in enumerate((a, b, c))
-            ]
-            square = rel[0] * rel[0] + rel[1] * rel[1] + rel[2] * rel[2]
-            length = square * lax.rsqrt(jnp.maximum(square, 1e-30))
-            scaled = (length - natural) * (HALF / natural)
-            pen = pen_of(a, b, c, word, bit, backward, place)
-            weight = 1.0 + jnp.tanh(pen - scaled)
-            pulled = weight * scaled
-            direction = lax.rsqrt(square + DIRECTION_EPS)
-            along_ref[place] = weight * direction
-            across_ref[place] = pulled * direction
-            moved = moved + pulled
-            other = other + (pen if kinds == "volume" else weight)
-        totals = totals + moved * (0.5 * natural / HALF)
-        if kinds == "volume":
-            lost = (PEN * len(bonds) - other) * (1.0 / LOST)
-            second = second + (len(bonds) - lost) * natural
-        else:
-            second = second + other * (0.5 * natural)
-    return totals, second
+    shape = (last - first, own_ref.shape[-1])
+
+    def layer(x, carry):
+        totals = jnp.zeros(shape, F32)
+        second = jnp.zeros(shape, F32)
+        for squared, bonds in CLASSES.items():
+            natural = math.sqrt(squared)
+            moved = jnp.zeros(shape, F32)
+            other = jnp.zeros(shape, F32)
+            for a, b, c, word, bit, backward, place in bonds:
+                rel = [
+                    rolled_ref[c + REACH, f, x + 3 + a, first + b : last + b] - own_ref[f, step + REACH, x]
+                    for f, step in enumerate((a, b, c))
+                ]
+                square = rel[0] * rel[0] + rel[1] * rel[1] + rel[2] * rel[2]
+                length = square * lax.rsqrt(jnp.maximum(square, 1e-30))
+                scaled = (length - natural) * (HALF / natural)
+                pen = pen_of(a, b, c, word, bit, backward, place, x)
+                weight = 1.0 + jnp.tanh(pen - scaled)
+                pulled = weight * scaled
+                square_ref[place, x] = square
+                along_ref[place, x] = weight
+                across_ref[place, x] = pulled
+                moved = moved + pulled
+                other = other + (pen if kinds == "volume" else weight)
+            totals = totals + moved * (0.5 * natural / HALF)
+            if kinds == "volume":
+                lost = (PEN * len(bonds) - other) * (1.0 / LOST)
+                second = second + (len(bonds) - lost) * natural
+            else:
+                second = second + other * (0.5 * natural)
+        out_ref[0, x] = totals
+        out_ref[1, x] = second
+        return carry
+
+    lax.fori_loop(0, 3, layer, 0)
+    return out_ref[0], out_ref[1]
 
 
 def cut_ratio(ratio_ref, to_odd_ref, to_even_ref, rows):
@@ -271,7 +287,7 @@
     return sum(rows + 2 * outer_rows(distance) for distance in range(1, 4))
 
 
-def first_kernel(side_ref, sent_ref, kept_ref, odd_ref, even_ref, v_hbm, rolled_ref, pen_ref, along_ref, across_ref, ratio_ref, to_odd_ref, to_even_ref, volume_ref, v_ref, mine_ref, field_ref, nb_ref, word_ref, sem):
+def first_kernel(side_ref, sent_ref, kept_ref, odd_ref, even_ref, v_hbm, rolled_ref, pen_ref, square_ref, along_ref, across_ref, ratio_ref, to_odd_ref, to_even_ref, volume_ref, v_ref, mine_ref, field_ref, nb_ref, word_ref, sums_ref, sem):
     copy = pltpu.make_async_copy(v_hbm, v_ref, sem)
     copy.start()
     rows = sent_ref.shape[-2]
@@ -283,33 +299,36 @@
     fill_moving(tile_of, ALL_STRIPS, odd_ref, even_ref, field_ref, rolled_ref, mine_ref, cells, region)
     bone = lay(field_ref.at[0], 3, tile_of, ALL_STRIPS, odd_ref, even_ref)
     void = jnp.where(bone == 0.0, -1, 0)
-    lane = lax.broadcasted_iota(jnp.int32, void.shape, 2)
     for c in range(-REACH, REACH + 1):
-        turned = shifted(void, c)
+        part = layers_read(c)
+        turned = shifted(void[part], c)
         if c != 0:
-            turned = jnp.where((lane + c >= 0) & (lane + c < depth), turned, -1)
-        nb_ref[c + REACH] = turned
+            lane = lax.broadcasted_iota(jnp.int32, turned.shape, 2) + c
+            turned = jnp.where((lane >= 0) & (lane < depth), turned, -1)
+        nb_ref[c + REACH, part] = turned
     for w in range(4):
         words = lay(field_ref.at[1 + w % 2], 4 + w, tile_of, ALL_STRIPS, odd_ref, even_ref)
         words = words[0 : 2 * cells].astype(jnp.int32)
         for c in range(-REACH, REACH + 1):
-            word_ref[c + REACH, w] = shifted(words, c) | nb_ref[c + REACH, 0 : 2 * cells]
+            part = layers_read(c, w)
+            if part is not None:
+                word_ref[c + REACH, w, part] = shifted(words[part], c) | nb_ref[c + REACH, part]
 
     first, last = region
 
-    def pen_of(a, b, c, word, bit, backward, place):
+    def pen_of(a, b, c, word, bit, backward, place, x):
         if backward:
-            words = word_ref[c + REACH, word, cells + a : 2 * cells + a, first + b : last + b]
+            words = word_ref[c + REACH, word, x + 3 + a, first + b : last + b]
             hit = words & (1 << bit)
         else:
-            words = word_ref[REACH, word, cells : 2 * cells, first:last]
-            far = nb_ref[c + REACH, cells + a : 2 * cells + a, first + b : last + b]
+            words = word_ref[REACH, word, x + 3, first:last]
+            far = nb_ref[c + REACH, x + 3 + a, first + b : last + b]
             hit = (words & (1 << bit)) | far
         pen = jnp.where(hit == 0, PEN, PEN - LOST)
-        pen_ref[place] = pen
+        pen_ref[place, x] = pen
         return pen
 
-    totals, volume = bond_pass(rolled_ref, mine_ref, pen_of, along_ref, across_ref, cells, region, "volume")
+    totals, volume = bond_pass(rolled_ref, mine_ref, pen_of, square_ref, along_ref, across_ref, sums_ref, region, "volume")
     solid = jnp.where(nb_ref[REACH, cells : 2 * cells, first:last] == 0, 1.0, 0.0)
     volume = jnp.maximum(volume * solid, 1.0)
     inverse = 1.0 / volume
@@ -322,7 +341,7 @@
     copy.wait()
 
 
-def later_kernel(side_ref, own_ref, odd_ref, even_ref, pen_ref, volume_ref, rolled_ref, along_ref, across_ref, ratio_ref, to_odd_ref, to_even_ref, damage_ref, mine_ref, field_ref):
+def later_kernel(side_ref, own_ref, odd_ref, even_ref, pen_ref, volume_ref, rolled_ref, square_ref, along_ref, across_ref, ratio_ref, to_odd_ref, to_even_ref, damage_ref, mine_ref, field_ref, sums_ref):
     rows = own_ref.shape[-2]
     cells = pen_ref.shape[1]
     half = rows // 2
@@ -330,10 +349,10 @@
     tile_of = tiles(side_ref, own_ref, None)
     fill_moving(tile_of, MOVING_STRIPS, odd_ref, even_ref, field_ref, rolled_ref, mine_ref, cells, region)
 
-    def pen_of(a, b, c, word, bit, backward, place):
-        return pen_ref[place]
-
-    totals, held = bond_pass(rolled_ref, mine_ref, pen_of, along_ref, across_ref, cells, region, "weight")
+    def pen_of(a, b, c, word, bit, backward, place, x):
+        return pen_ref[place, x]
+
+    totals, held = bond_pass(rolled_ref, mine_ref, pen_of, square_ref, along_ref, across_ref, sums_ref, region, "weight")
     volume = volume_ref[0]
     solid = volume_ref[1]
     inverse = 1.0 / volume
@@ -344,7 +363,7 @@
     damage_ref[...] = damage[:, half : half + rows]
 
 
-def forces(total, inner, rolled_ref, along_ref, across_ref, scaled_ref, inverse_ref, rows):
+def forces(total, inner, rolled_ref, square_ref, along_ref, across_ref, scaled_ref, inverse_ref, rows):
     half = rows // 2
     mine = slice(half, half + rows)
     for x in range(3):
@@ -358,6 +377,7 @@
                 far = (c + REACH, x + 3 + a, slice(half + b, half + rows + b))
                 magnitude = along_ref[place, x, mine] * (scaled + scaled_ref[far])
                 magnitude = magnitude + across_ref[place, x, mine] * (inverse + inverse_ref[far])
+                magnitude = magnitude * lax.rsqrt(square_ref[place, x, mine] + DIRECTION_EPS)
                 for f, step in enumerate((a, b, c)):
                     rel = rolled_ref[c + REACH, f, x + 3 + a, rows + b : 2 * rows + b] - here[f]
                     if step:
@@ -394,38 +414,38 @@
     return [[jnp.zeros((rows, depth), F32) for _ in range(3)] for _ in range(3)]
 
 
-def inner_kernel(rolled_ref, along_ref, across_ref, ratio_ref, held_ref, part_ref, scaled_ref, inverse_ref):
+def inner_kernel(rolled_ref, square_ref, along_ref, across_ref, ratio_ref, held_ref, part_ref, scaled_ref, inverse_ref):
     rows, depth = part_ref.shape[2:]
     fill_inner(scaled_ref, ratio_ref[0])
     if held_ref is None:
         held_ref = inverse_ref
         fill_inner(inverse_ref, ratio_ref[1])
-    total = forces(start_total(rows, depth), True, rolled_ref, along_ref, across_ref, scaled_ref, held_ref, rows)
+    total = forces(start_total(rows, depth), True, rolled_ref, square_ref, along_ref, across_ref, scaled_ref, held_ref, rows)
     for f in range(3):
         for x in range(3):
             part_ref[f, x] = total[f][x]
 
 
-def first_inner_kernel(rolled_ref, along_ref, across_ref, ratio_ref, part_ref, scaled_ref, inverse_ref):
-    inner_kernel(rolled_ref, along_ref, across_ref, ratio_ref, None, part_ref, scaled_ref, inverse_ref)
-
-
-def last_inner_kernel(rolled_ref, along_ref, across_ref, ratio_ref, inverse_ref, part_ref, scaled_ref):
-    inner_kernel(rolled_ref, along_ref, across_ref, ratio_ref, inverse_ref, part_ref, scaled_ref, None)
-
-
-def outer_forces(rolled_ref, along_ref, across_ref, scaled_ref, inverse_ref, part_ref, rows):
+def first_inner_kernel(rolled_ref, square_ref, along_ref, across_ref, ratio_ref, part_ref, scaled_ref, inverse_ref):
+    inner_kernel(rolled_ref, square_ref, along_ref, across_ref, ratio_ref, None, part_ref, scaled_ref, inverse_ref)
+
+
+def last_inner_kernel(rolled_ref, square_ref, along_ref, across_ref, ratio_ref, inverse_ref, part_ref, scaled_ref):
+    inner_kernel(rolled_ref, square_ref, along_ref, across_ref, ratio_ref, inverse_ref, part_ref, scaled_ref, None)
+
+
+def outer_forces(rolled_ref, square_ref, along_ref, across_ref, scaled_ref, inverse_ref, part_ref, rows):
     total = [[part_ref[f, x] for x in range(3)] for f in range(3)]
-    return forces(total, False, rolled_ref, along_ref, across_ref, scaled_ref, inverse_ref, rows)
-
-
-def move_kernel(rolled_ref, along_ref, across_ref, ratio_ref, part_ref, odd_ref, even_ref, volume_ref, sent_ref, v_ref, u_out, v_out, inverse_ref, scaled_ref, field_ref):
+    return forces(total, False, rolled_ref, square_ref, along_ref, across_ref, scaled_ref, inverse_ref, rows)
+
+
+def move_kernel(rolled_ref, square_ref, along_ref, across_ref, ratio_ref, part_ref, odd_ref, even_ref, volume_ref, sent_ref, v_ref, u_out, v_out, inverse_ref, scaled_ref, field_ref):
     rows = v_ref.shape[2]
     half = rows // 2
     for f, target in ((0, scaled_ref), (1, inverse_ref)):
         fill_outer(target, field_ref.at[f], f, odd_ref, even_ref, rows)
         fill_inner(target, ratio_ref[f])
-    total = outer_forces(rolled_ref, along_ref, across_ref, scaled_ref, inverse_ref, part_ref, rows)
+    total = outer_forces(rolled_ref, square_ref, along_ref, across_ref, scaled_ref, inverse_ref, part_ref, rows)
     for f in range(3):
         for x in range(3):
             speed = v_ref[f, x] + TIME_STEP * (total[f][x] * volume_ref[1, x, half : half + rows])
@@ -433,13 +453,13 @@
             u_out[3 * f + x] = sent_ref[3 * f + x] + TIME_STEP * speed
 
 
-def last_kernel(rolled_ref, along_ref, across_ref, ratio_ref, part_ref, odd_ref, even_ref, volume_ref, v_ref, inverse_ref, damage_ref, v_out, damage_out, scaled_ref, field_ref):
+def last_kernel(rolled_ref, square_ref, along_ref, across_ref, ratio_ref, part_ref, odd_ref, even_ref, volume_ref, v_ref, inverse_ref, damage_ref, v_out, damage_out, scaled_ref, field_ref):
     rows = v_ref.shape[2]
     half = rows // 2
     damage_out[...] = damage_ref[...]
     fill_outer(scaled_ref, field_ref, 0, odd_ref, even_ref, rows)
     scaled_ref[REACH, 3:6] = ratio_ref[0]
-    total = outer_forces(rolled_ref, along_ref, across_ref, scaled_ref, inverse_ref, part_ref, rows)
+    total = outer_forces(rolled_ref, square_ref, along_ref, across_ref, scaled_ref, inverse_ref, part_ref, rows)
     for f in range(3):
         for x in range(3):
             v_out[f, x] = v_ref[f, x] + TIME_STEP * (total[f][x] * volume_ref[1, x, half : half + rows])
@@ -478,10 +498,11 @@
     )
     bonds = (BONDS, cells, region, depth)
     crossing = ratio_rows(rows)
-    rolled, pen, along, across, ratio, to_odd, to_even, volume, speed = call(
+    rolled, pen, square, along, across, ratio, to_odd, to_even, volume, speed = call(
         first_kernel,
         (
             vmem(turns, 3, layers, tall, depth),
+            vmem(*bonds),
             vmem(*bonds),
             vmem(*bonds),
             vmem(*bonds),
@@ -501,6 +522,7 @@
             vmem(3, layers, tall, depth),
             vmem(turns, layers, tall, depth, dtype=jnp.int32),
             vmem(turns, 4, 2 * cells, tall, depth, dtype=jnp.int32),
+            vmem(2, cells, region, depth),
             pltpu.SemaphoreType.DMA(()),
         ),
         hbm=(5,),
@@ -508,12 +530,20 @@
     arrived = both(to_odd, to_even, "gx")
     wide_ratio = vmem(turns, layers, region, depth)
     part = call(
-        first_inner_kernel, vmem(3, cells, rows, depth), rolled, along, across, ratio, scratch=(wide_ratio, wide_ratio)
+        first_inner_kernel,
+        vmem(3, cells, rows, depth),
+        rolled,
+        square,
+        along,
+        across,
+        ratio,
+        scratch=(wide_ratio, wide_ratio),
     )
     moved, speed, inverse = call(
         move_kernel,
         (vmem(3 * cells, rows, depth), vmem(3, cells, rows, depth), wide_ratio),
         rolled,
+        square,
         along,
         across,
         ratio,
@@ -530,10 +560,11 @@
         moved,
         *both(moved, moved, "gx"),
     )
-    rolled, along, across, ratio, to_odd, to_even, damage = call(
+    rolled, square, along, across, ratio, to_odd, to_even, damage = call(
         later_kernel,
         (
             vmem(turns, 3, layers, tall, depth),
+            vmem(*bonds),
             vmem(*bonds),
             vmem(*bonds),
             vmem(1, cells, region, depth),
@@ -549,16 +580,26 @@
         scratch=(
             vmem(3, turns, cells, region, depth),
             vmem(3, layers, tall, depth),
+            vmem(2, cells, region, depth),
         ),
     )
     arrived = both(to_odd, to_even, "gx")
     part = call(
-        last_inner_kernel, vmem(3, cells, rows, depth), rolled, along, across, ratio, inverse, scratch=(wide_ratio,)
+        last_inner_kernel,
+        vmem(3, cells, rows, depth),
+        rolled,
+        square,
+        along,
+        across,
+        ratio,
+        inverse,
+        scratch=(wide_ratio,),
     )
     return call(
         last_kernel,
         (hbm((3, cells, rows, depth), F32), hbm((cells, rows, depth), F32)),
         rolled,
+        square,
         along,
         across,
         ratio,

time: 70.7 us -> 69.6 us (0.984)
  Pallas kernels: 10.8 us -> 9.98 us
    pallas_call x9, Pallas kernels: 10.8 us -> 9.98 us  [call(): pl.pallas_call(kernel, out_shape=outs, in_specs=[pl.BlockSpec(memory_spac...]
where the time goes in v1:
time: 69.6 us; the launch traced here: 69.3 us
  starting transfers between devices  36.6 us (53%)
  waiting for transfers between devices  21.9 us (31%)
  Pallas kernels  9.98 us (14%)
  between operations  0.78 us (1%)
    ppermute x12, starting transfers between devices, pairwise(): return lax.ppermute(values, axis, pairs)  36.6 us
    ppermute x12, waiting for transfers between devices, pairwise(): return lax.ppermute(values, axis, pairs)  21.9 us
    pallas_call x9, Pallas kernels, call(): pl.pallas_call(kernel, out_shape=outs, in_specs=[pl.BlockSpec(memory_spac...  9.98 us
  transfers between devices with their start and end apart: 12, of which 7 were waited for; matrix products, arithmetic and copies ran while one was open for 0% of the time, Pallas kernels for 2%

profile of v1, /device:TPU:38, one launch (start us, length us, event | category | flops | bytes accessed | tf_op | source)
XLA Modules:
  0.0 69.3 jit_solution(1937816175276172139)
XLA Ops:
  0.6 0.9 %shard_map.59 = (f32[19,8,128]{2,1,0:T(8,128)S(1)}, f32[5,8,128]{2,1,0:T(8,128)S(1)}) custom-call(f32[3,3,8,128]{3,2,1,0:T(8,128)} %u_ref.1, s32[3,8,128]{2,1,0:T(8,128)} %bone_ref.1, s32[4,3,8,128]{3,2,1,0:T(8,128)} %broken_ref.1), custom_call_target="tpu_custom_call" | custom-call | tf_op jit(solution)/shard_map/pallas_call | solution.py:87
  1.5 1.7 %collective-permute-start.1 = (f32[19,8,128]{2,1,0:T(8,128)S(1)}, f32[19,8,128]{2,1,0:T(8,128)S(1)}, u32[]{:S(2)}, u32[]{:S(2)}) collective-permute-start(f32[19,8,128]{2,1,0:T(8,128)S(1)} %get-tuple-element.31.sent_ref), channel_id=1, source_target_pairs={{0,4},{4,0},{8,12},{12,8},{16,20},{20,16},{24,28},{28,24},{32,36},... | collective-permute-start | bytes 233480 | tf_op jit(solution)/shard_map/ppermute | solution.py:76
  3.2 9.2 %collective-permute-start = (f32[19,8,128]{2,1,0:T(8,128)S(1)}, f32[19,8,128]{2,1,0:T(8,128)S(1)}, u32[]{:S(2)}, u32[]{:S(2)}) collective-permute-start(f32[19,8,128]{2,1,0:T(8,128)S(1)} %get-tuple-element.31.sent_ref), channel_id=1, source_target_pairs={{4,8},{8,4},{12,16},{16,12},{20,24},{24,20},{28,32},{32,28},{36,40... | collective-permute-start | bytes 233480 | tf_op jit(solution)/shard_map/ppermute | solution.py:76
  12.4 3.7 %collective-permute-done.odd_ref = f32[19,8,128]{2,1,0:T(8,128)S(1)} collective-permute-done((f32[19,8,128]{2,1,0:T(8,128)S(1)}, f32[19,8,128]{2,1,0:T(8,128)S(1)}, u32[]{:S(2)}, u32[]{:S(2)}) %collective-permute-start) | collective-permute-done | bytes 77856 | tf_op jit(solution)/shard_map/ppermute | solution.py:76
  16.1 1.9 %collective-permute-start.2 = (f32[281,128]{1,0:T(8,128)S(1)}, f32[281,128]{1,0:T(8,128)S(1)}, u32[]{:S(2)}, u32[]{:S(2)}) collective-permute-start(f32[281,128]{1,0:T(8,128)S(1)} %get-tuple-element.34), channel_id=1, source_target_pairs={{1,2},{2,1},{5,6},{6,5},{9,10},{10,9},{13,14},{14,13},{17,18},{18,... | collective-permute-start | bytes 431624 | tf_op jit(solution)/shard_map/ppermute | solution.py:76
  18.1 0.1 collective-permute-start.3
  18.2 4.4 %collective-permute-done.2.odd_ref = f32[281,128]{1,0:T(8,128)S(1)} collective-permute-done((f32[281,128]{1,0:T(8,128)S(1)}, f32[281,128]{1,0:T(8,128)S(1)}, u32[]{:S(2)}, u32[]{:S(2)}) %collective-permute-start.2) | collective-permute-done | bytes 143904 | tf_op jit(solution)/shard_map/ppermute | solution.py:76
  22.6 3.1 %shard_map.61 = (f32[7,3,9,24,128]{4,3,2,1,0:T(8,128)S(1)}, f32[122,3,16,128]{3,2,1,0:T(8,128)S(1)}, f32[122,3,16,128]{3,2,1,0:T(8,128)S(1)}, f32[122,3,16,128]{...) custom-call(f32[2,19,8,128]{3,2,1,0:T(8,128)S(1)} %get-tuple-element, ...), custom_call_target="tpu_custom_call" | custom-call | tf_op jit(solution)/shard_map/pallas_call | solution.py:87
  25.8 7.7 %collective-permute-start.4 = (f32[64,128]{1,0:T(8,128)S(1)}, f32[64,128]{1,0:T(8,128)S(1)}, u32[]{:S(2)}, u32[]{:S(2)}) collective-permute-start(f32[64,128]{1,0:T(8,128)S(1)} %get-tuple-element.41), channel_id=1, source_target_pairs={{4,8},{8,4},{12,16},{16,12},{20,24},{24,20},{28,32},{32,28},{36,40... | collective-permute-start | bytes 98312 | tf_op jit(solution)/shard_map/ppermute | solution.py:76
  33.4 0.1 collective-permute-start.5
  33.5 0.8 %shard_map.62.part_ref = f32[3,3,8,128]{3,2,1,0:T(8,128)S(1)} custom-call(f32[7,3,9,24,128]{4,3,2,1,0:T(8,128)S(1)} %get-tuple-element.36.rolled_ref, f32[122,3,16,128]{3,2,1,0:T(8,128)S(1)} %get-tuple-element.37.square_ref, f32[122,3,16,128]{3,2,1,0:T(8,128)S(1)} %get-tuple-element.38.along_ref, f32[122,3,16,128]{3,2,1,0:T(8,128)S(1)} %get-tuple-element.39.across_ref, ...), custom_call_target="tpu_custom_call" | custom-call | tf_op jit(solution)/shard_map/pallas_call | solution.py:87
  34.4 2.3 %collective-permute-done.4.odd_ref = f32[64,128]{1,0:T(8,128)S(1)} collective-permute-done((f32[64,128]{1,0:T(8,128)S(1)}, f32[64,128]{1,0:T(8,128)S(1)}, u32[]{:S(2)}, u32[]{:S(2)}) %collective-permute-start.4) | collective-permute-done | bytes 32800 | tf_op jit(solution)/shard_map/ppermute | solution.py:76
  36.7 0.8 %collective-permute-done.5.even_ref = f32[64,128]{1,0:T(8,128)S(1)} collective-permute-done((f32[64,128]{1,0:T(8,128)S(1)}, f32[64,128]{1,0:T(8,128)S(1)}, u32[]{:S(2)}, u32[]{:S(2)}) %collective-permute-start.5) | collective-permute-done | bytes 32800 | tf_op jit(solution)/shard_map/ppermute | solution.py:76
  37.4 0.7 shard_map.63
  38.1 0.1 collective-permute-start.7
  38.2 6.9 %collective-permute-start.6 = (f32[9,8,128]{2,1,0:T(8,128)S(1)}, f32[9,8,128]{2,1,0:T(8,128)S(1)}, u32[]{:S(2)}, u32[]{:S(2)}) collective-permute-start(f32[9,8,128]{2,1,0:T(8,128)S(1)} %get-tuple-element.45.own_ref), channel_id=1, source_target_pairs={{4,8},{8,4},{12,16},{16,12},{20,24},{24,20},{28,32},{32,28},{36,40... | collective-permute-start | bytes 110600 | tf_op jit(solution)/shard_map/ppermute | solution.py:76
  45.2 4.1 %collective-permute-done.6.odd_ref = f32[9,8,128]{2,1,0:T(8,128)S(1)} collective-permute-done((f32[9,8,128]{2,1,0:T(8,128)S(1)}, f32[9,8,128]{2,1,0:T(8,128)S(1)}, u32[]{:S(2)}, u32[]{:S(2)}) %collective-permute-start.6) | collective-permute-done | bytes 36896 | tf_op jit(solution)/shard_map/ppermute | solution.py:76
  49.3 1.9 %collective-permute-start.8 = (f32[132,128]{1,0:T(8,128)S(1)}, f32[132,128]{1,0:T(8,128)S(1)}, u32[]{:S(2)}, u32[]{:S(2)}) collective-permute-start(f32[132,128]{1,0:T(8,128)S(1)} %get-tuple-element.47), channel_id=1, source_target_pairs={{1,2},{2,1},{5,6},{6,5},{9,10},{10,9},{13,14},{14,13},{17,18},{18,... | collective-permute-start | bytes 202760 | tf_op jit(solution)/shard_map/ppermute | solution.py:76
  51.3 3.6 %collective-permute-done.8.odd_ref = f32[132,128]{1,0:T(8,128)S(1)} collective-permute-done((f32[132,128]{1,0:T(8,128)S(1)}, f32[132,128]{1,0:T(8,128)S(1)}, u32[]{:S(2)}, u32[]{:S(2)}) %collective-permute-start.8) | collective-permute-done | bytes 67616 | tf_op jit(solution)/shard_map/ppermute | solution.py:76
  54.9 2.5 %shard_map.65 = (f32[7,3,9,24,128]{4,3,2,1,0:T(8,128)S(1)}, f32[122,3,16,128]{3,2,1,0:T(8,128)S(1)}, f32[122,3,16,128]{3,2,1,0:T(8,128)S(1)}, f32[122,3,16,128]{...) custom-call(f32[2,9,8,128]{3,2,1,0:T(8,128)S(1)} %get-tuple-element., ...), custom_call_target="tpu_custom_call" | custom-call | tf_op jit(solution)/shard_map/pallas_call | solution.py:87
  57.4 6.9 %collective-permute-start.10 = (f32[32,128]{1,0:T(8,128)S(1)}, f32[32,128]{1,0:T(8,128)S(1)}, u32[]{:S(2)}, u32[]{:S(2)}) collective-permute-start(f32[32,128]{1,0:T(8,128)S(1)} %get-tuple-element.56), channel_id=1, source_target_pairs={{4,8},{8,4},{12,16},{16,12},{20,24},{24,20},{28,32},{32,28},{36,40... | collective-permute-start | bytes 49160 | tf_op jit(solution)/shard_map/ppermute | solution.py:76
  64.4 0.7 %shard_map.66.part_ref = f32[3,3,8,128]{3,2,1,0:T(8,128)S(1)} custom-call(f32[7,3,9,24,128]{4,3,2,1,0:T(8,128)S(1)} %get-tuple-element.50.rolled_ref, f32[122,3,16,128]{3,2,1,0:T(8,128)S(1)} %get-tuple-element.51.square_ref, f32[122,3,16,128]{3,2,1,0:T(8,128)S(1)} %get-tuple-element.52.along_ref, f32[122,3,16,128]{3,2,1,0:T(8,128)S(1)} %get-tuple-element.53.across_ref, ...), custom_call_target="tpu_custom_call" | custom-call | tf_op jit(solution)/shard_map/pallas_call | solution.py:87
  65.1 3.0 %collective-permute-done.10.odd_ref = f32[32,128]{1,0:T(8,128)S(1)} collective-permute-done((f32[32,128]{1,0:T(8,128)S(1)}, f32[32,128]{1,0:T(8,128)S(1)}, u32[]{:S(2)}, u32[]{:S(2)}) %collective-permute-start.10) | collective-permute-done | bytes 16416 | tf_op jit(solution)/shard_map/ppermute | solution.py:76
  68.1 1.2 %shard_map.67 = (f32[3,3,8,128]{3,2,1,0:T(8,128)}, f32[3,8,128]{2,1,0:T(8,128)}) custom-call(f32[7,3,9,24,128]{4,3,2,1,0:T(8,128)S(1)} %get-tuple-element.50.rolled_ref, f32[122,3,16,128]{3,2,1,0:T(8,128)S(1)} %get-tuple-element.51.square_ref, f32[122,3,16,128]{3,2,1,0:T(8,128)S(1)} %get-tuple-element.52.along_ref, ...), custom_call_target="tpu_custom_call" | custom-call | tf_op jit(solution)/shard_map/pallas_call | solution.py:87
  (9 shorter events, 0.3 us)
Async XLA Ops:
  1.5 10.9 %collective-permute-start.1 = (f32[19,8,128]{2,1,0:T(8,128)S(1)}, f32[19,8,128]{2,1,0:T(8,128)S(1)}, u32[]{:S(2)}, u32[]{:S(2)}) collective-permute-start(f32[19,8,128]{2,1,0:T(8,128)S(1)} %get-tuple-element.31.sent_ref), channel_id=1, source_target_pairs={{0,4},{4,0},{8,12},{12,8},{16,20},{20,16},{24,28},{28,24},{32,36},... | collective-permute-start | bytes 233480 | tf_op jit(solution)/shard_map/ppermute | solution.py:76
  3.2 12.9 %collective-permute-start = (f32[19,8,128]{2,1,0:T(8,128)S(1)}, f32[19,8,128]{2,1,0:T(8,128)S(1)}, u32[]{:S(2)}, u32[]{:S(2)}) collective-permute-start(f32[19,8,128]{2,1,0:T(8,128)S(1)} %get-tuple-element.31.sent_ref), channel_id=1, source_target_pairs={{4,8},{8,4},{12,16},{16,12},{20,24},{24,20},{28,32},{32,28},{36,40... | collective-permute-start | bytes 233480 | tf_op jit(solution)/shard_map/ppermute | solution.py:76
  16.1 6.5 %collective-permute-start.2 = (f32[281,128]{1,0:T(8,128)S(1)}, f32[281,128]{1,0:T(8,128)S(1)}, u32[]{:S(2)}, u32[]{:S(2)}) collective-permute-start(f32[281,128]{1,0:T(8,128)S(1)} %get-tuple-element.34), channel_id=1, source_target_pairs={{1,2},{2,1},{5,6},{6,5},{9,10},{10,9},{13,14},{14,13},{17,18},{18,... | collective-permute-start | bytes 431624 | tf_op jit(solution)/shard_map/ppermute | solution.py:76
  18.1 4.5 %collective-permute-start.3 = (f32[281,128]{1,0:T(8,128)S(1)}, f32[281,128]{1,0:T(8,128)S(1)}, u32[]{:S(2)}, u32[]{:S(2)}) collective-permute-start(f32[281,128]{1,0:T(8,128)S(1)} %get-tuple-element.35), channel_id=1, source_target_pairs={{0,1},{1,0},{2,3},{3,2},{4,5},{5,4},{6,7},{7,6},{8,9},{9,8},{10,11... | collective-permute-start | bytes 431624 | tf_op jit(solution)/shard_map/ppermute | solution.py:76
  25.8 10.9 %collective-permute-start.4 = (f32[64,128]{1,0:T(8,128)S(1)}, f32[64,128]{1,0:T(8,128)S(1)}, u32[]{:S(2)}, u32[]{:S(2)}) collective-permute-start(f32[64,128]{1,0:T(8,128)S(1)} %get-tuple-element.41), channel_id=1, source_target_pairs={{4,8},{8,4},{12,16},{16,12},{20,24},{24,20},{28,32},{32,28},{36,40... | collective-permute-start | bytes 98312 | tf_op jit(solution)/shard_map/ppermute | solution.py:76
  33.4 4.0 %collective-permute-start.5 = (f32[64,128]{1,0:T(8,128)S(1)}, f32[64,128]{1,0:T(8,128)S(1)}, u32[]{:S(2)}, u32[]{:S(2)}) collective-permute-start(f32[64,128]{1,0:T(8,128)S(1)} %get-tuple-element.42), channel_id=1, source_target_pairs={{0,4},{4,0},{8,12},{12,8},{16,20},{20,16},{24,28},{28,24},{32,36},... | collective-permute-start | bytes 98312 | tf_op jit(solution)/shard_map/ppermute | solution.py:76
  38.1 7.0 %collective-permute-start.7 = (f32[9,8,128]{2,1,0:T(8,128)S(1)}, f32[9,8,128]{2,1,0:T(8,128)S(1)}, u32[]{:S(2)}, u32[]{:S(2)}) collective-permute-start(f32[9,8,128]{2,1,0:T(8,128)S(1)} %get-tuple-element.45.own_ref), channel_id=1, source_target_pairs={{0,4},{4,0},{8,12},{12,8},{16,20},{20,16},{24,28},{28,24},{32,36},... | collective-permute-start | bytes 110600 | tf_op jit(solution)/shard_map/ppermute | solution.py:76
  38.2 11.0 %collective-permute-start.6 = (f32[9,8,128]{2,1,0:T(8,128)S(1)}, f32[9,8,128]{2,1,0:T(8,128)S(1)}, u32[]{:S(2)}, u32[]{:S(2)}) collective-permute-start(f32[9,8,128]{2,1,0:T(8,128)S(1)} %get-tuple-element.45.own_ref), channel_id=1, source_target_pairs={{4,8},{8,4},{12,16},{16,12},{20,24},{24,20},{28,32},{32,28},{36,40... | collective-permute-start | bytes 110600 | tf_op jit(solution)/shard_map/ppermute | solution.py:76
  49.3 5.6 %collective-permute-start.8 = (f32[132,128]{1,0:T(8,128)S(1)}, f32[132,128]{1,0:T(8,128)S(1)}, u32[]{:S(2)}, u32[]{:S(2)}) collective-permute-start(f32[132,128]{1,0:T(8,128)S(1)} %get-tuple-element.47), channel_id=1, source_target_pairs={{1,2},{2,1},{5,6},{6,5},{9,10},{10,9},{13,14},{14,13},{17,18},{18,... | collective-permute-start | bytes 202760 | tf_op jit(solution)/shard_map/ppermute | solution.py:76
  51.2 3.7 %collective-permute-start.9 = (f32[132,128]{1,0:T(8,128)S(1)}, f32[132,128]{1,0:T(8,128)S(1)}, u32[]{:S(2)}, u32[]{:S(2)}) collective-permute-start(f32[132,128]{1,0:T(8,128)S(1)} %get-tuple-element.48), channel_id=1, source_target_pairs={{0,1},{1,0},{2,3},{3,2},{4,5},{5,4},{6,7},{7,6},{8,9},{9,8},{10,11... | collective-permute-start | bytes 202760 | tf_op jit(solution)/shard_map/ppermute | solution.py:76
  57.4 10.8 %collective-permute-start.10 = (f32[32,128]{1,0:T(8,128)S(1)}, f32[32,128]{1,0:T(8,128)S(1)}, u32[]{:S(2)}, u32[]{:S(2)}) collective-permute-start(f32[32,128]{1,0:T(8,128)S(1)} %get-tuple-element.56), channel_id=1, source_target_pairs={{4,8},{8,4},{12,16},{16,12},{20,24},{24,20},{28,32},{32,28},{36,40... | collective-permute-start | bytes 49160 | tf_op jit(solution)/shard_map/ppermute | solution.py:76
  64.3 3.9 %collective-permute-start.11 = (f32[32,128]{1,0:T(8,128)S(1)}, f32[32,128]{1,0:T(8,128)S(1)}, u32[]{:S(2)}, u32[]{:S(2)}) collective-permute-start(f32[32,128]{1,0:T(8,128)S(1)} %get-tuple-element.57), channel_id=1, source_target_pairs={{0,4},{4,0},{8,12},{12,8},{16,20},{20,16},{24,28},{28,24},{32,36},... | collective-permute-start | bytes 49160 | tf_op jit(solution)/shard_map/ppermute | solution.py:76

commit v2 on v1

--- a/solution.py
+++ b/solution.py
@@ -67,6 +67,17 @@
     if c == 0:
         reach.append(0)
     return slice(3 + min(reach), 6 + max(reach)) if reach else None
+
+
+SIDE = (-3, -2, -1, 3, 4, 5)
+PAIRS = [(bond, x) for bond in DIRECTED for x in range(3)]
+INNER = {(bond[-1], x): None for bond, x in PAIRS if 0 <= x + bond[0] < 3}
+INNER = {key: n for n, key in enumerate(INNER)}
+OUTER = {(bond[-1], x): None for bond, x in PAIRS if not 0 <= x + bond[0] < 3}
+OUTER = {key: n for n, key in enumerate(OUTER)}
+ROWS_Y = 6
+BEYOND = (0, 5, 5, 3)
+BEYOND_RATIO = (0, 2, 2, 0)
 
 
 def pairwise(values, axis, odd):
@@ -177,13 +188,6 @@
     side_ref[0] = jnp.where(even, odd_ref[...], even_ref[...])
     side_ref[1] = jnp.where(even, even_ref[...], odd_ref[...])
     cut_strips(tiles(side_ref, sent_ref, kept_ref), ALL_STRIPS, to_odd_ref, to_even_ref)
-
-
-def widen_moving_kernel(own_ref, odd_ref, even_ref, side_ref, to_odd_ref, to_even_ref):
-    even = is_even("gx")
-    side_ref[0] = jnp.where(even, odd_ref[...], even_ref[...])
-    side_ref[1] = jnp.where(even, even_ref[...], odd_ref[...])
-    cut_strips(tiles(side_ref, own_ref, None), MOVING_STRIPS, to_odd_ref, to_even_ref)
 
 
 def tiles(side_ref, own_ref, kept_ref):
@@ -341,28 +345,6 @@
     copy.wait()
 
 
-def later_kernel(side_ref, own_ref, odd_ref, even_ref, pen_ref, volume_ref, rolled_ref, square_ref, along_ref, across_ref, ratio_ref, to_odd_ref, to_even_ref, damage_ref, mine_ref, field_ref, sums_ref):
-    rows = own_ref.shape[-2]
-    cells = pen_ref.shape[1]
-    half = rows // 2
-    region = (half, half + 2 * rows)
-    tile_of = tiles(side_ref, own_ref, None)
-    fill_moving(tile_of, MOVING_STRIPS, odd_ref, even_ref, field_ref, rolled_ref, mine_ref, cells, region)
-
-    def pen_of(a, b, c, word, bit, backward, place, x):
-        return pen_ref[place, x]
-
-    totals, held = bond_pass(rolled_ref, mine_ref, pen_of, square_ref, along_ref, across_ref, sums_ref, region, "weight")
-    volume = volume_ref[0]
-    solid = volume_ref[1]
-    inverse = 1.0 / volume
-    dilatation = 3.0 * (totals * solid) / volume
-    ratio_ref[0] = dilatation * inverse * (0.5 * BULK_TERM)
-    cut_ratio(ratio_ref, to_odd_ref, to_even_ref, rows)
-    damage = 1.0 - (held * solid) / volume
-    damage_ref[...] = damage[:, half : half + rows]
-
-
 def forces(total, inner, rolled_ref, square_ref, along_ref, across_ref, scaled_ref, inverse_ref, rows):
     half = rows // 2
     mine = slice(half, half + rows)
@@ -430,16 +412,12 @@
     inner_kernel(rolled_ref, square_ref, along_ref, across_ref, ratio_ref, None, part_ref, scaled_ref, inverse_ref)
 
 
-def last_inner_kernel(rolled_ref, square_ref, along_ref, across_ref, ratio_ref, inverse_ref, part_ref, scaled_ref):
-    inner_kernel(rolled_ref, square_ref, along_ref, across_ref, ratio_ref, inverse_ref, part_ref, scaled_ref, None)
-
-
 def outer_forces(rolled_ref, square_ref, along_ref, across_ref, scaled_ref, inverse_ref, part_ref, rows):
     total = [[part_ref[f, x] for x in range(3)] for f in range(3)]
     return forces(total, False, rolled_ref, square_ref, along_ref, across_ref, scaled_ref, inverse_ref, rows)
 
 
-def move_kernel(rolled_ref, square_ref, along_ref, across_ref, ratio_ref, part_ref, odd_ref, even_ref, volume_ref, sent_ref, v_ref, u_out, v_out, inverse_ref, scaled_ref, field_ref):
+def move_kernel(rolled_ref, square_ref, along_ref, across_ref, ratio_ref, part_ref, odd_ref, even_ref, volume_ref, sent_ref, v_ref, u_out, v_out, inverse_ref, to_odd_ref, to_even_ref, scaled_ref, field_ref):
     rows = v_ref.shape[2]
     half = rows // 2
     for f, target in ((0, scaled_ref), (1, inverse_ref)):
@@ -450,16 +428,226 @@
         for x in range(3):
             speed = v_ref[f, x] + TIME_STEP * (total[f][x] * volume_ref[1, x, half : half + rows])
             v_out[f, x] = speed
-            u_out[3 * f + x] = sent_ref[3 * f + x] + TIME_STEP * speed
-
-
-def last_kernel(rolled_ref, square_ref, along_ref, across_ref, ratio_ref, part_ref, odd_ref, even_ref, volume_ref, v_ref, inverse_ref, damage_ref, v_out, damage_out, scaled_ref, field_ref):
+            u_out[f, x] = sent_ref[3 * f + x] + TIME_STEP * speed
+    cut_y(lambda f, x: u_out[f, x], 3, to_odd_ref, to_even_ref)
+
+
+def strips_x(fields, rows, beyond):
+    placed, start = {}, 0
+    for f in range(fields):
+        for distance in range(1, 4):
+            if f >= 4 and word_reach()[f - 4] < distance:
+                continue
+            count = rows + 2 * beyond[distance]
+            placed[f, distance] = (start, count, beyond[distance])
+            start += count
+    return placed, start
+
+
+def cut_y(value_of, fields, odd_ref, even_ref):
+    even = is_even("gy")
+    for f in range(fields):
+        for x in range(3):
+            tile = value_of(f, x)
+            first, last = tile[0:ROWS_Y], tile[tile.shape[0] - ROWS_Y :]
+            part = slice((3 * f + x) * ROWS_Y, (3 * f + x + 1) * ROWS_Y)
+            odd_ref[part] = jnp.where(even, first, last)
+            even_ref[part] = jnp.where(even, last, first)
+
+
+def cut_x(source_ref, fields, rows, beyond, base, odd_ref, even_ref):
+    even = is_even("gx")
+    for (f, distance), (start, count, more) in strips_x(fields, rows, beyond)[0].items():
+        part = slice(base - more, base + rows + more)
+        upper, lower = source_ref[f, 3 - distance, part], source_ref[f, distance - 1, part]
+        odd_ref[start : start + count] = jnp.where(even, lower, upper)
+        even_ref[start : start + count] = jnp.where(even, upper, lower)
+
+
+def lay_side(field_ref, f, fields, rows, beyond, base, odd_ref, even_ref):
+    even = is_even("gx")
+    field_ref[...] = jnp.zeros(field_ref.shape, F32)
+    placed = strips_x(fields, rows, beyond)[0]
+    for distance in range(1, 4):
+        if (f, distance) in placed:
+            start, count, more = placed[f, distance]
+            part = slice(base - more, base + rows + more)
+            from_odd, from_even = odd_ref[start : start + count], even_ref[start : start + count]
+            field_ref[3 - distance, part] = jnp.where(even, from_odd, from_even)
+            field_ref[2 + distance, part] = jnp.where(even, from_even, from_odd)
+    return field_ref[...]
+
+
+def outer_part(c):
+    return {0: slice(0, 6), 3: None}.get(abs(c), slice(1, 5))
+
+
+def widen_moved_kernel(own_ref, odd_ref, even_ref, tall_ref, to_odd_ref, to_even_ref):
+    even = is_even("gy")
+    fields, rows = own_ref.shape[0], own_ref.shape[2]
+    blank = jnp.zeros((rows - ROWS_Y, own_ref.shape[3]), F32)
+    for f in range(fields):
+        for x in range(3):
+            part = slice((3 * f + x) * ROWS_Y, (3 * f + x + 1) * ROWS_Y)
+            from_odd, from_even = odd_ref[part], even_ref[part]
+            tall_ref[f, x, 0 : rows - ROWS_Y] = blank
+            tall_ref[f, x, rows - ROWS_Y : rows] = jnp.where(even, from_odd, from_even)
+            tall_ref[f, x, rows : 2 * rows] = own_ref[f, x]
+            tall_ref[f, x, 2 * rows : 2 * rows + ROWS_Y] = jnp.where(even, from_even, from_odd)
+            tall_ref[f, x, 2 * rows + ROWS_Y :] = blank
+    cut_x(tall_ref, fields, rows, BEYOND, rows, to_odd_ref, to_even_ref)
+
+
+def region_of(rows):
+    return rows // 2, rows // 2 + 2 * rows
+
+
+def split_pass(places, far_of, own_ref, pen_of, square_ref, along_ref, across_ref, sums_ref, begun_ref, kinds):
+    shape = own_ref.shape[3:]
+    for x in range(3):
+        totals = jnp.zeros(shape, F32) if begun_ref is None else begun_ref[0, x]
+        second = jnp.zeros(shape, F32) if begun_ref is None else begun_ref[1, x]
+        for squared, bonds in CLASSES.items():
+            natural = math.sqrt(squared)
+            held = [bond for bond in bonds if (bond[-1], x) in places]
+            if not held:
+                continue
+            moved = jnp.zeros(shape, F32)
+            other = jnp.zeros(shape, F32)
+            for bond in held:
+                a, b, c = bond[:3]
+                n = places[bond[-1], x]
+                rel = [far_of(c, f, x + a, b) - own_ref[f, step + REACH, x] for f, step in enumerate((a, b, c))]
+                square = rel[0] * rel[0] + rel[1] * rel[1] + rel[2] * rel[2]
+                length = square * lax.rsqrt(jnp.maximum(square, 1e-30))
+                scaled = (length - natural) * (HALF / natural)
+                pen = pen_of(bond, n, x)
+                weight = 1.0 + jnp.tanh(pen - scaled)
+                pulled = weight * scaled
+                square_ref[n] = square
+                along_ref[n] = weight
+                across_ref[n] = pulled
+                moved = moved + pulled
+                other = other + (pen if kinds == "volume" else weight)
+            totals = totals + moved * (0.5 * natural / HALF)
+            if kinds == "volume":
+                lost = (PEN * len(held) - other) * (1.0 / LOST)
+                second = second + (len(held) - lost) * natural
+            else:
+                second = second + other * (0.5 * natural)
+        sums_ref[0, x] = totals
+        sums_ref[1, x] = second
+
+
+def fill_inner_moving(tall_ref, rolled_ref, mine_ref):
+    first, last = region_of(tall_ref.shape[2] // 3)
+    for f in range(3):
+        field = tall_ref[f]
+        for c in range(-REACH, REACH + 1):
+            rolled_ref[c + REACH, f] = shifted(field, c)
+        here = tall_ref[f, :, first:last]
+        for step in range(-REACH, REACH + 1):
+            mine_ref[f, step + REACH] = here - float(step)
+
+
+def fill_outer_moving(odd_ref, even_ref, fields, field_ref, rolled_ref):
+    rows = field_ref.shape[2] // 3
+    for f in range(3):
+        field = lay_side(field_ref.at[f], f, fields, rows, BEYOND, rows, odd_ref, even_ref)
+        for c in range(-REACH, REACH + 1):
+            part = outer_part(c)
+            if part is not None:
+                rolled_ref[c + REACH, f, part] = shifted(field[part], c)
+
+
+def inner_far(rolled_ref):
+    first, last = region_of(rolled_ref.shape[3] // 3)
+    return lambda c, f, layer, b: rolled_ref[c + REACH, f, layer, first + b : last + b]
+
+
+def outer_far(rolled_ref):
+    first, last = region_of(rolled_ref.shape[3] // 3)
+    return lambda c, f, layer, b: rolled_ref[c + REACH, f, SIDE.index(layer), first + b : last + b]
+
+
+def later_inside_kernel(tall_ref, pen_ref, rolled_ref, mine_ref, square_ref, along_ref, across_ref, sums_ref):
+    fill_inner_moving(tall_ref, rolled_ref, mine_ref)
+    split_pass(INNER, inner_far(rolled_ref), mine_ref, lambda bond, n, x: pen_ref[bond[-1], x], square_ref, along_ref, across_ref, sums_ref, None, "weight")
+
+
+def later_kernel(odd_ref, even_ref, mine_ref, pen_ref, begun_ref, volume_ref, rolled_ref, square_ref, along_ref, across_ref, ratio_ref, to_odd_ref, to_even_ref, damage_ref, field_ref, sums_ref):
+    rows = field_ref.shape[2] // 3
+    half = rows // 2
+    fill_outer_moving(odd_ref, even_ref, 3, field_ref, rolled_ref)
+    split_pass(OUTER, outer_far(rolled_ref), mine_ref, lambda bond, n, x: pen_ref[bond[-1], x], square_ref, along_ref, across_ref, sums_ref, begun_ref, "weight")
+    volume = volume_ref[0]
+    solid = volume_ref[1]
+    inverse = 1.0 / volume
+    dilatation = 3.0 * (sums_ref[0] * solid) / volume
+    ratio_ref[0] = dilatation * inverse * (0.5 * BULK_TERM)
+    cut_x(ratio_ref, 1, rows, BEYOND_RATIO, half, to_odd_ref, to_even_ref)
+    damage = 1.0 - (sums_ref[1] * solid) / volume
+    damage_ref[...] = damage[:, half : half + rows]
+
+
+def split_forces(total, places, index, rolled_ref, here_ref, square_ref, along_ref, across_ref, ratio_ref, held_ref, scaled_ref, inverse_ref):
+    rows = here_ref.shape[3] // 3
+    half = rows // 2
+    mine = slice(half, half + rows)
+    for x in range(3):
+        scaled = ratio_ref[0, x, mine]
+        inverse = held_ref[1, x, mine]
+        here = [here_ref[REACH, f, x, rows : 2 * rows] for f in range(3)]
+        for a, b, c, word, bit, backward, place in DIRECTED:
+            if (place, x) not in places:
+                continue
+            n = places[place, x]
+            far = (c + REACH, index(x + a), slice(half + b, half + rows + b))
+            magnitude = along_ref[n, mine] * (scaled + scaled_ref[far])
+            magnitude = magnitude + across_ref[n, mine] * (inverse + inverse_ref[c + REACH, x + 3 + a, far[2]])
+            magnitude = magnitude * lax.rsqrt(square_ref[n, mine] + DIRECTION_EPS)
+            for f, step in enumerate((a, b, c)):
+                rel = rolled_ref[c + REACH, f, index(x + a), rows + b : 2 * rows + b] - here[f]
+                if step:
+                    rel = rel + float(step)
+                total[f][x] = total[f][x] + magnitude * rel
+    return total
+
+
+def fill_own(target_ref, own):
+    for c in range(-REACH, REACH + 1):
+        target_ref[c + REACH] = shifted(own, c)
+
+
+def fill_side(target_ref, field_ref, f, fields, odd_ref, even_ref, rows):
+    field = lay_side(field_ref, f, fields, rows, BEYOND_RATIO, rows // 2, odd_ref, even_ref)
+    for c in range(-REACH, REACH + 1):
+        part = outer_part(c)
+        if part is not None:
+            target_ref[c + REACH, part] = shifted(field[part], c)
+
+
+def inside_forces(rolled_ref, square_ref, along_ref, across_ref, ratio_ref, held_ref, scaled_ref, inverse_ref, part_ref):
+    rows, depth = part_ref.shape[2:]
+    total = [[jnp.zeros((rows, depth), F32) for _ in range(3)] for _ in range(3)]
+    total = split_forces(total, INNER, lambda layer: layer, rolled_ref, rolled_ref, square_ref, along_ref, across_ref, ratio_ref, held_ref, scaled_ref, inverse_ref)
+    for f in range(3):
+        for x in range(3):
+            part_ref[f, x] = total[f][x]
+
+
+def last_inside_kernel(rolled_ref, square_ref, along_ref, across_ref, ratio_ref, held_ref, inverse_ref, part_ref, scaled_ref):
+    fill_own(scaled_ref, ratio_ref[0])
+    inside_forces(rolled_ref, square_ref, along_ref, across_ref, ratio_ref, held_ref, scaled_ref, inverse_ref, part_ref)
+
+
+def last_kernel(odd_ref, even_ref, rolled_ref, inside_ref, square_ref, along_ref, across_ref, ratio_ref, held_ref, part_ref, volume_ref, v_ref, inverse_ref, damage_ref, v_out, damage_out, scaled_ref, field_ref):
     rows = v_ref.shape[2]
     half = rows // 2
     damage_out[...] = damage_ref[...]
-    fill_outer(scaled_ref, field_ref, 0, odd_ref, even_ref, rows)
-    scaled_ref[REACH, 3:6] = ratio_ref[0]
-    total = outer_forces(rolled_ref, square_ref, along_ref, across_ref, scaled_ref, inverse_ref, part_ref, rows)
+    fill_side(scaled_ref, field_ref, 0, 1, odd_ref, even_ref, rows)
+    total = [[part_ref[f, x] for x in range(3)] for f in range(3)]
+    total = split_forces(total, OUTER, SIDE.index, rolled_ref, inside_ref, square_ref, along_ref, across_ref, ratio_ref, held_ref, scaled_ref, inverse_ref)
     for f in range(3):
         for x in range(3):
             v_out[f, x] = v_ref[f, x] + TIME_STEP * (total[f][x] * volume_ref[1, x, half : half + rows])
@@ -539,9 +727,9 @@
         ratio,
         scratch=(wide_ratio, wide_ratio),
     )
-    moved, speed, inverse = call(
+    moved, speed, inverse, *to = call(
         move_kernel,
-        (vmem(3 * cells, rows, depth), vmem(3, cells, rows, depth), wide_ratio),
+        (vmem(3, cells, rows, depth), vmem(3, cells, rows, depth), wide_ratio) + (vmem(3 * 3 * ROWS_Y, depth),) * 2,
         rolled,
         square,
         along,
@@ -554,62 +742,52 @@
         speed,
         scratch=(wide_ratio, vmem(2, 6, region, depth)),
     )
-    side, to_odd, to_even = call(
-        widen_moving_kernel,
-        (vmem(2, len(MOVING), rows, depth), vmem(MOVING_ROWS, depth), vmem(MOVING_ROWS, depth)),
-        moved,
-        *both(moved, moved, "gx"),
-    )
-    rolled, square, along, across, ratio, to_odd, to_even, damage = call(
+    sides = len(SIDE)
+    block = vmem(3, cells, rows, depth)
+    in_bonds, out_bonds = vmem(len(INNER), region, depth), vmem(len(OUTER), region, depth)
+    in_rolled, out_rolled = vmem(turns, 3, cells, tall, depth), vmem(turns, 3, sides, tall, depth)
+    in_ratio, out_ratio = vmem(turns, cells, region, depth), vmem(turns, sides, region, depth)
+    mine_shape = vmem(3, turns, cells, region, depth)
+    two = vmem(2, cells, region, depth)
+
+    def strips(fields, beyond):
+        return (vmem(strips_x(fields, rows, beyond)[1], depth),) * 2
+
+    tall_moved, *to = call(
+        widen_moved_kernel, (vmem(3, cells, tall, depth),) + strips(3, BEYOND), moved, *both(*to, "gy")
+    )
+    arrived = both(*to, "gx")
+    inside, mine, *in_held, begun = call(
+        later_inside_kernel, (in_rolled, mine_shape) + (in_bonds,) * 3 + (two,), tall_moved, pen
+    )
+    held_ratio = ratio
+    rolled, *out_held, ratio, to_odd, to_even, damage = call(
         later_kernel,
-        (
-            vmem(turns, 3, layers, tall, depth),
-            vmem(*bonds),
-            vmem(*bonds),
-            vmem(*bonds),
-            vmem(1, cells, region, depth),
-            vmem(crossing, depth),
-            vmem(crossing, depth),
-            vmem(cells, rows, depth),
-        ),
-        side,
-        moved,
-        *both(to_odd, to_even, "gy"),
+        (out_rolled,) + (out_bonds,) * 3 + (vmem(1, cells, region, depth),) + strips(1, BEYOND_RATIO) + (vmem(cells, rows, depth),),
+        *arrived,
+        mine,
         pen,
+        begun,
         volume,
-        scratch=(
-            vmem(3, turns, cells, region, depth),
-            vmem(3, layers, tall, depth),
-            vmem(2, cells, region, depth),
-        ),
+        scratch=(vmem(3, sides, tall, depth), two),
     )
     arrived = both(to_odd, to_even, "gx")
-    part = call(
-        last_inner_kernel,
-        vmem(3, cells, rows, depth),
-        rolled,
-        square,
-        along,
-        across,
-        ratio,
-        inverse,
-        scratch=(wide_ratio,),
-    )
+    part = call(last_inside_kernel, block, inside, *in_held, ratio, held_ratio, inverse, scratch=(in_ratio,))
     return call(
         last_kernel,
         (hbm((3, cells, rows, depth), F32), hbm((cells, rows, depth), F32)),
+        *arrived,
         rolled,
-        square,
-        along,
-        across,
+        inside,
+        *out_held,
         ratio,
+        held_ratio,
         part,
-        *arrived,
         volume,
         speed,
         inverse,
         damage,
-        scratch=(wide_ratio, vmem(6, region, depth)),
+        scratch=(out_ratio, vmem(sides, region, depth)),
     )
 
 

time: 69.6 us -> 68.6 us (0.986)
    pallas_call x9 -> x10, Pallas kernels: 9.98 us -> 10.1 us  [call(): pl.pallas_call(kernel, out_shape=outs, in_specs=[pl.BlockSpec(memory_spac...]
  transfers between devices with their start and end apart: 12 -> 12, of which waited for: 7 -> 7; matrix products, arithmetic and copies ran while one was open for 0% -> 0% of each run, Pallas kernels for 2% -> 5%
where the time goes in v2:
time: 68.6 us; the launch traced here: 68.3 us
  starting transfers between devices  36.1 us (53%)
  waiting for transfers between devices  21.3 us (31%)
  Pallas kernels  10.1 us (15%)
  between operations  0.77 us (1%)
    ppermute x12, starting transfers between devices, pairwise(): return lax.ppermute(values, axis, pairs)  36.1 us
    ppermute x12, waiting for transfers between devices, pairwise(): return lax.ppermute(values, axis, pairs)  21.3 us
    pallas_call x10, Pallas kernels, call(): pl.pallas_call(kernel, out_shape=outs, in_specs=[pl.BlockSpec(memory_spac...  10.1 us
  transfers between devices with their start and end apart: 12, of which 7 were waited for; matrix products, arithmetic and copies ran while one was open for 0% of the time, Pallas kernels for 5%

profile of v2, /device:TPU:38, one launch (start us, length us, event | category | flops | bytes accessed | tf_op | source)
XLA Modules:
  0.0 68.3 jit_solution(14358855344604572303)
XLA Ops:
  0.6 0.9 %shard_map.59 = (f32[19,8,128]{2,1,0:T(8,128)S(1)}, f32[5,8,128]{2,1,0:T(8,128)S(1)}) custom-call(f32[3,3,8,128]{3,2,1,0:T(8,128)} %u_ref.1, s32[3,8,128]{2,1,0:T(8,128)} %bone_ref.1, s32[4,3,8,128]{3,2,1,0:T(8,128)} %broken_ref.1), custom_call_target="tpu_custom_call" | custom-call | tf_op jit(solution)/shard_map/pallas_call | solution.py:98
  1.5 1.7 %collective-permute-start.1 = (f32[19,8,128]{2,1,0:T(8,128)S(1)}, f32[19,8,128]{2,1,0:T(8,128)S(1)}, u32[]{:S(2)}, u32[]{:S(2)}) collective-permute-start(f32[19,8,128]{2,1,0:T(8,128)S(1)} %get-tuple-element.39.sent_ref), channel_id=1, source_target_pairs={{0,4},{4,0},{8,12},{12,8},{16,20},{20,16},{24,28},{28,24},{32,36},... | collective-permute-start | bytes 233480 | tf_op jit(solution)/shard_map/ppermute | solution.py:87
  3.2 9.2 %collective-permute-start = (f32[19,8,128]{2,1,0:T(8,128)S(1)}, f32[19,8,128]{2,1,0:T(8,128)S(1)}, u32[]{:S(2)}, u32[]{:S(2)}) collective-permute-start(f32[19,8,128]{2,1,0:T(8,128)S(1)} %get-tuple-element.39.sent_ref), channel_id=1, source_target_pairs={{4,8},{8,4},{12,16},{16,12},{20,24},{24,20},{28,32},{32,28},{36,40... | collective-permute-start | bytes 233480 | tf_op jit(solution)/shard_map/ppermute | solution.py:87
  12.4 3.7 %collective-permute-done.odd_ref = f32[19,8,128]{2,1,0:T(8,128)S(1)} collective-permute-done((f32[19,8,128]{2,1,0:T(8,128)S(1)}, f32[19,8,128]{2,1,0:T(8,128)S(1)}, u32[]{:S(2)}, u32[]{:S(2)}) %collective-permute-start) | collective-permute-done | bytes 77856 | tf_op jit(solution)/shard_map/ppermute | solution.py:87
  16.1 1.9 %collective-permute-start.2 = (f32[281,128]{1,0:T(8,128)S(1)}, f32[281,128]{1,0:T(8,128)S(1)}, u32[]{:S(2)}, u32[]{:S(2)}) collective-permute-start(f32[281,128]{1,0:T(8,128)S(1)} %get-tuple-element.42), channel_id=1, source_target_pairs={{1,2},{2,1},{5,6},{6,5},{9,10},{10,9},{13,14},{14,13},{17,18},{18,... | collective-permute-start | bytes 431624 | tf_op jit(solution)/shard_map/ppermute | solution.py:87
  18.1 0.1 collective-permute-start.3
  18.2 4.4 %collective-permute-done.2.odd_ref = f32[281,128]{1,0:T(8,128)S(1)} collective-permute-done((f32[281,128]{1,0:T(8,128)S(1)}, f32[281,128]{1,0:T(8,128)S(1)}, u32[]{:S(2)}, u32[]{:S(2)}) %collective-permute-start.2) | collective-permute-done | bytes 143904 | tf_op jit(solution)/shard_map/ppermute | solution.py:87
  22.6 3.2 %shard_map.61 = (f32[7,3,9,24,128]{4,3,2,1,0:T(8,128)S(1)}, f32[122,3,16,128]{3,2,1,0:T(8,128)S(1)}, f32[122,3,16,128]{3,2,1,0:T(8,128)S(1)}, f32[122,3,16,128]{...) custom-call(f32[2,19,8,128]{3,2,1,0:T(8,128)S(1)} %get-tuple-element, ...), custom_call_target="tpu_custom_call" | custom-call | tf_op jit(solution)/shard_map/pallas_call | solution.py:98
  25.8 7.7 %collective-permute-start.4 = (f32[64,128]{1,0:T(8,128)S(1)}, f32[64,128]{1,0:T(8,128)S(1)}, u32[]{:S(2)}, u32[]{:S(2)}) collective-permute-start(f32[64,128]{1,0:T(8,128)S(1)} %get-tuple-element.49), channel_id=1, source_target_pairs={{4,8},{8,4},{12,16},{16,12},{20,24},{24,20},{28,32},{32,28},{36,40... | collective-permute-start | bytes 98312 | tf_op jit(solution)/shard_map/ppermute | solution.py:87
  33.6 0.8 %shard_map.62.part_ref = f32[3,3,8,128]{3,2,1,0:T(8,128)S(1)} custom-call(f32[7,3,9,24,128]{4,3,2,1,0:T(8,128)S(1)} %get-tuple-element.44.rolled_ref, f32[122,3,16,128]{3,2,1,0:T(8,128)S(1)} %get-tuple-element.45.square_ref, f32[122,3,16,128]{3,2,1,0:T(8,128)S(1)} %get-tuple-element.46.along_ref, f32[122,3,16,128]{3,2,1,0:T(8,128)S(1)} %get-tuple-element.47.across_ref, ...), custom_call_target="tpu_custom_call" | custom-call | tf_op jit(solution)/shard_map/pallas_call | solution.py:98
  34.4 2.3 %collective-permute-done.4.odd_ref = f32[64,128]{1,0:T(8,128)S(1)} collective-permute-done((f32[64,128]{1,0:T(8,128)S(1)}, f32[64,128]{1,0:T(8,128)S(1)}, u32[]{:S(2)}, u32[]{:S(2)}) %collective-permute-start.4) | collective-permute-done | bytes 32800 | tf_op jit(solution)/shard_map/ppermute | solution.py:87
  36.7 0.8 %collective-permute-done.5.even_ref = f32[64,128]{1,0:T(8,128)S(1)} collective-permute-done((f32[64,128]{1,0:T(8,128)S(1)}, f32[64,128]{1,0:T(8,128)S(1)}, u32[]{:S(2)}, u32[]{:S(2)}) %collective-permute-start.5) | collective-permute-done | bytes 32800 | tf_op jit(solution)/shard_map/ppermute | solution.py:87
  37.5 0.7 shard_map.63
  38.1 1.9 %collective-permute-start.6 = (f32[54,128]{1,0:T(8,128)S(1)}, f32[54,128]{1,0:T(8,128)S(1)}, u32[]{:S(2)}, u32[]{:S(2)}) collective-permute-start(f32[54,128]{1,0:T(8,128)S(1)} %get-tuple-element.54), channel_id=1, source_target_pairs={{1,2},{2,1},{5,6},{6,5},{9,10},{10,9},{13,14},{14,13},{17,18},{18,... | collective-permute-start | bytes 82952 | tf_op jit(solution)/shard_map/ppermute | solution.py:87
  40.1 0.1 collective-permute-start.7
  40.2 3.2 %collective-permute-done.6.odd_ref = f32[54,128]{1,0:T(8,128)S(1)} collective-permute-done((f32[54,128]{1,0:T(8,128)S(1)}, f32[54,128]{1,0:T(8,128)S(1)}, u32[]{:S(2)}, u32[]{:S(2)}) %collective-permute-start.6) | collective-permute-done | bytes 27680 | tf_op jit(solution)/shard_map/ppermute | solution.py:87
  43.4 6.9 %collective-permute-start.8 = (f32[150,128]{1,0:T(8,128)S(1)}, f32[150,128]{1,0:T(8,128)S(1)}, u32[]{:S(2)}, u32[]{:S(2)}) collective-permute-start(f32[150,128]{1,0:T(8,128)S(1)} %get-tuple-element.56), channel_id=1, source_target_pairs={{4,8},{8,4},{12,16},{16,12},{20,24},{24,20},{28,32},{32,28},{36,40... | collective-permute-start | bytes 230408 | tf_op jit(solution)/shard_map/ppermute | solution.py:87
  50.4 1.4 %shard_map.65 = (f32[7,3,3,24,128]{4,3,2,1,0:T(8,128)S(1)}, f32[3,7,3,16,128]{4,3,2,1,0:T(8,128)S(1)}, f32[226,16,128]{2,1,0:T(8,128)S(1)}, f32[226,16,128]{2,1,...) custom-call(f32[3,3,24,128]{3,2,1,0:T(8,128)S(1)} %get-tuple-element.58.tall_ref, ...), custom_call_target="tpu_custom_call" | custom-call | tf_op jit(solution)/shard_map/pallas_call | solution.py:98
  51.9 3.5 %collective-permute-done.8.odd_ref = f32[150,128]{1,0:T(8,128)S(1)} collective-permute-done((f32[150,128]{1,0:T(8,128)S(1)}, f32[150,128]{1,0:T(8,128)S(1)}, u32[]{:S(2)}, u32[]{:S(2)}) %collective-permute-start.8) | collective-permute-done | bytes 76832 | tf_op jit(solution)/shard_map/ppermute | solution.py:87
  55.3 1.0 %shard_map.66 = (f32[7,3,6,24,128]{4,3,2,1,0:T(8,128)S(1)}, f32[140,16,128]{2,1,0:T(8,128)S(1)}, f32[140,16,128]{2,1,0:T(8,128)S(1)}, f32[140,16,128]{2,1,0:T(8,...) custom-call(f32[150,128]{1,0:T(8,128)S(1)} %collective-permute-done., ...), custom_call_target="tpu_custom_call" | custom-call | tf_op jit(solution)/shard_map/pallas_call | solution.py:98
  56.4 6.4 %collective-permute-start.10 = (f32[32,128]{1,0:T(8,128)S(1)}, f32[32,128]{1,0:T(8,128)S(1)}, u32[]{:S(2)}, u32[]{:S(2)}) collective-permute-start(f32[32,128]{1,0:T(8,128)S(1)} %get-tuple-element.62), channel_id=1, source_target_pairs={{4,8},{8,4},{12,16},{16,12},{20,24},{24,20},{28,32},{32,28},{36,40... | collective-permute-start | bytes 49160 | tf_op jit(solution)/shard_map/ppermute | solution.py:87
  62.8 0.8 %shard_map.67.part_ref = f32[3,3,8,128]{3,2,1,0:T(8,128)S(1)} custom-call(f32[7,3,3,24,128]{4,3,2,1,0:T(8,128)S(1)} %get-tuple-element.65.rolled_ref.inside_ref, f32[226,16,128]{2,1,0:T(8,128)S(1)} %get-tuple-element.70.square_ref, f32[226,16,128]{2,1,0:T(8,128)S(1)} %get-tuple-element.71.along_ref, f32[226,16,128]{2,1,0:T(8,128)S(1)} %get-tuple-element.72.across_ref, ...), custom_call_target="tpu_custom_call" | custom-call | tf_op jit(solution)/shard_map/pallas_call | solution.py:98
  63.6 3.5 %collective-permute-done.10.odd_ref = f32[32,128]{1,0:T(8,128)S(1)} collective-permute-done((f32[32,128]{1,0:T(8,128)S(1)}, f32[32,128]{1,0:T(8,128)S(1)}, u32[]{:S(2)}, u32[]{:S(2)}) %collective-permute-start.10) | collective-permute-done | bytes 16416 | tf_op jit(solution)/shard_map/ppermute | solution.py:87
  67.1 1.2 %shard_map.68 = (f32[3,3,8,128]{3,2,1,0:T(8,128)}, f32[3,8,128]{2,1,0:T(8,128)}) custom-call(f32[32,128]{1,0:T(8,128)S(1)} %collective-permute-done.10.odd_ref, f32[32,128]{1,0:T(8,128)S(1)} %collective-permute-done.11.even_ref, f32[7,3,6,24,128]{4,3,2,1,0:T(8,128)S(1)} %get-tuple-element.64.rolled_ref, ...), custom_call_target="tpu_custom_call" | custom-call | tf_op jit(solution)/shard_map/pallas_call | solution.py:98
  (10 shorter events, 0.4 us)
Async XLA Ops:
  1.5 10.9 %collective-permute-start.1 = (f32[19,8,128]{2,1,0:T(8,128)S(1)}, f32[19,8,128]{2,1,0:T(8,128)S(1)}, u32[]{:S(2)}, u32[]{:S(2)}) collective-permute-start(f32[19,8,128]{2,1,0:T(8,128)S(1)} %get-tuple-element.39.sent_ref), channel_id=1, source_target_pairs={{0,4},{4,0},{8,12},{12,8},{16,20},{20,16},{24,28},{28,24},{32,36},... | collective-permute-start | bytes 233480 | tf_op jit(solution)/shard_map/ppermute | solution.py:87
  3.2 12.9 %collective-permute-start = (f32[19,8,128]{2,1,0:T(8,128)S(1)}, f32[19,8,128]{2,1,0:T(8,128)S(1)}, u32[]{:S(2)}, u32[]{:S(2)}) collective-permute-start(f32[19,8,128]{2,1,0:T(8,128)S(1)} %get-tuple-element.39.sent_ref), channel_id=1, source_target_pairs={{4,8},{8,4},{12,16},{16,12},{20,24},{24,20},{28,32},{32,28},{36,40... | collective-permute-start | bytes 233480 | tf_op jit(solution)/shard_map/ppermute | solution.py:87
  16.1 6.5 %collective-permute-start.2 = (f32[281,128]{1,0:T(8,128)S(1)}, f32[281,128]{1,0:T(8,128)S(1)}, u32[]{:S(2)}, u32[]{:S(2)}) collective-permute-start(f32[281,128]{1,0:T(8,128)S(1)} %get-tuple-element.42), channel_id=1, source_target_pairs={{1,2},{2,1},{5,6},{6,5},{9,10},{10,9},{13,14},{14,13},{17,18},{18,... | collective-permute-start | bytes 431624 | tf_op jit(solution)/shard_map/ppermute | solution.py:87
  18.1 4.5 %collective-permute-start.3 = (f32[281,128]{1,0:T(8,128)S(1)}, f32[281,128]{1,0:T(8,128)S(1)}, u32[]{:S(2)}, u32[]{:S(2)}) collective-permute-start(f32[281,128]{1,0:T(8,128)S(1)} %get-tuple-element.43), channel_id=1, source_target_pairs={{0,1},{1,0},{2,3},{3,2},{4,5},{5,4},{6,7},{7,6},{8,9},{9,8},{10,11... | collective-permute-start | bytes 431624 | tf_op jit(solution)/shard_map/ppermute | solution.py:87
  25.8 10.9 %collective-permute-start.4 = (f32[64,128]{1,0:T(8,128)S(1)}, f32[64,128]{1,0:T(8,128)S(1)}, u32[]{:S(2)}, u32[]{:S(2)}) collective-permute-start(f32[64,128]{1,0:T(8,128)S(1)} %get-tuple-element.49), channel_id=1, source_target_pairs={{4,8},{8,4},{12,16},{16,12},{20,24},{24,20},{28,32},{32,28},{36,40... | collective-permute-start | bytes 98312 | tf_op jit(solution)/shard_map/ppermute | solution.py:87
  33.5 4.0 %collective-permute-start.5 = (f32[64,128]{1,0:T(8,128)S(1)}, f32[64,128]{1,0:T(8,128)S(1)}, u32[]{:S(2)}, u32[]{:S(2)}) collective-permute-start(f32[64,128]{1,0:T(8,128)S(1)} %get-tuple-element.50), channel_id=1, source_target_pairs={{0,4},{4,0},{8,12},{12,8},{16,20},{20,16},{24,28},{28,24},{32,36},... | collective-permute-start | bytes 98312 | tf_op jit(solution)/shard_map/ppermute | solution.py:87
  38.1 5.2 %collective-permute-start.6 = (f32[54,128]{1,0:T(8,128)S(1)}, f32[54,128]{1,0:T(8,128)S(1)}, u32[]{:S(2)}, u32[]{:S(2)}) collective-permute-start(f32[54,128]{1,0:T(8,128)S(1)} %get-tuple-element.54), channel_id=1, source_target_pairs={{1,2},{2,1},{5,6},{6,5},{9,10},{10,9},{13,14},{14,13},{17,18},{18,... | collective-permute-start | bytes 82952 | tf_op jit(solution)/shard_map/ppermute | solution.py:87
  40.1 3.3 %collective-permute-start.7 = (f32[54,128]{1,0:T(8,128)S(1)}, f32[54,128]{1,0:T(8,128)S(1)}, u32[]{:S(2)}, u32[]{:S(2)}) collective-permute-start(f32[54,128]{1,0:T(8,128)S(1)} %get-tuple-element.55), channel_id=1, source_target_pairs={{0,1},{1,0},{2,3},{3,2},{4,5},{5,4},{6,7},{7,6},{8,9},{9,8},{10,11... | collective-permute-start | bytes 82952 | tf_op jit(solution)/shard_map/ppermute | solution.py:87
  43.4 12.0 %collective-permute-start.8 = (f32[150,128]{1,0:T(8,128)S(1)}, f32[150,128]{1,0:T(8,128)S(1)}, u32[]{:S(2)}, u32[]{:S(2)}) collective-permute-start(f32[150,128]{1,0:T(8,128)S(1)} %get-tuple-element.56), channel_id=1, source_target_pairs={{4,8},{8,4},{12,16},{16,12},{20,24},{24,20},{28,32},{32,28},{36,40... | collective-permute-start | bytes 230408 | tf_op jit(solution)/shard_map/ppermute | solution.py:87
  50.3 5.0 %collective-permute-start.9 = (f32[150,128]{1,0:T(8,128)S(1)}, f32[150,128]{1,0:T(8,128)S(1)}, u32[]{:S(2)}, u32[]{:S(2)}) collective-permute-start(f32[150,128]{1,0:T(8,128)S(1)} %get-tuple-element.57), channel_id=1, source_target_pairs={{0,4},{4,0},{8,12},{12,8},{16,20},{20,16},{24,28},{28,24},{32,36},... | collective-permute-start | bytes 230408 | tf_op jit(solution)/shard_map/ppermute | solution.py:87
  56.4 10.7 %collective-permute-start.10 = (f32[32,128]{1,0:T(8,128)S(1)}, f32[32,128]{1,0:T(8,128)S(1)}, u32[]{:S(2)}, u32[]{:S(2)}) collective-permute-start(f32[32,128]{1,0:T(8,128)S(1)} %get-tuple-element.62), channel_id=1, source_target_pairs={{4,8},{8,4},{12,16},{16,12},{20,24},{24,20},{28,32},{32,28},{36,40... | collective-permute-start | bytes 49160 | tf_op jit(solution)/shard_map/ppermute | solution.py:87
  62.7 4.4 %collective-permute-start.11 = (f32[32,128]{1,0:T(8,128)S(1)}, f32[32,128]{1,0:T(8,128)S(1)}, u32[]{:S(2)}, u32[]{:S(2)}) collective-permute-start(f32[32,128]{1,0:T(8,128)S(1)} %get-tuple-element.63), channel_id=1, source_target_pairs={{0,4},{4,0},{8,12},{12,8},{16,20},{20,16},{24,28},{28,24},{32,36},... | collective-permute-start | bytes 49160 | tf_op jit(solution)/shard_map/ppermute | solution.py:87

commit v3 on v2

--- a/solution.py
+++ b/solution.py
@@ -387,9 +387,12 @@
         start += count
     field = field_ref[...]
     for c in range(-REACH, REACH + 1):
-        turned = shifted(field, c)
-        target_ref[c + REACH, 0:3] = turned[0:3]
-        target_ref[c + REACH, 6:9] = turned[3:6]
+        part = outer_part(c)
+        if part is not None:
+            turned = shifted(field[part], c)
+            side = turned.shape[0] // 2
+            target_ref[c + REACH, part.start : 3] = turned[:side]
+            target_ref[c + REACH, 6 : 3 + part.stop] = turned[side:]
 
 
 def start_total(rows, depth):
@@ -422,7 +425,8 @@
     half = rows // 2
     for f, target in ((0, scaled_ref), (1, inverse_ref)):
         fill_outer(target, field_ref.at[f], f, odd_ref, even_ref, rows)
-        fill_inner(target, ratio_ref[f])
+    scaled_ref[REACH, 3:6] = ratio_ref[0]
+    fill_inner(inverse_ref, ratio_ref[1])
     total = outer_forces(rolled_ref, square_ref, along_ref, across_ref, scaled_ref, inverse_ref, part_ref, rows)
     for f in range(3):
         for x in range(3):

time: 68.6 us -> 68.5 us (level)
  no operation moved by 1% of the time
where the time goes in v3:
time: 68.5 us; the launch traced here: 68.2 us
  starting transfers between devices  36.1 us (53%)
  waiting for transfers between devices  21.3 us (31%)
  Pallas kernels  9.96 us (15%)
  between operations  0.77 us (1%)
    ppermute x12, starting transfers between devices, pairwise(): return lax.ppermute(values, axis, pairs)  36.1 us
    ppermute x12, waiting for transfers between devices, pairwise(): return lax.ppermute(values, axis, pairs)  21.3 us
    pallas_call x10, Pallas kernels, call(): pl.pallas_call(kernel, out_shape=outs, in_specs=[pl.BlockSpec(memory_spac...  9.96 us
  transfers between devices with their start and end apart: 12, of which 7 were waited for; matrix products, arithmetic and copies ran while one was open for 0% of the time, Pallas kernels for 5%

profile of v3, /device:TPU:38, one launch (start us, length us, event | category | flops | bytes accessed | tf_op | source)
XLA Modules:
  0.0 68.2 jit_solution(2361132077837026085)
XLA Ops:
  0.6 0.9 %shard_map.59 = (f32[19,8,128]{2,1,0:T(8,128)S(1)}, f32[5,8,128]{2,1,0:T(8,128)S(1)}) custom-call(f32[3,3,8,128]{3,2,1,0:T(8,128)} %u_ref.1, s32[3,8,128]{2,1,0:T(8,128)} %bone_ref.1, s32[4,3,8,128]{3,2,1,0:T(8,128)} %broken_ref.1), custom_call_target="tpu_custom_call" | custom-call | tf_op jit(solution)/shard_map/pallas_call | solution.py:98
  1.5 1.7 %collective-permute-start.1 = (f32[19,8,128]{2,1,0:T(8,128)S(1)}, f32[19,8,128]{2,1,0:T(8,128)S(1)}, u32[]{:S(2)}, u32[]{:S(2)}) collective-permute-start(f32[19,8,128]{2,1,0:T(8,128)S(1)} %get-tuple-element.39.sent_ref), channel_id=1, source_target_pairs={{0,4},{4,0},{8,12},{12,8},{16,20},{20,16},{24,28},{28,24},{32,36},... | collective-permute-start | bytes 233480 | tf_op jit(solution)/shard_map/ppermute | solution.py:87
  3.2 9.2 %collective-permute-start = (f32[19,8,128]{2,1,0:T(8,128)S(1)}, f32[19,8,128]{2,1,0:T(8,128)S(1)}, u32[]{:S(2)}, u32[]{:S(2)}) collective-permute-start(f32[19,8,128]{2,1,0:T(8,128)S(1)} %get-tuple-element.39.sent_ref), channel_id=1, source_target_pairs={{4,8},{8,4},{12,16},{16,12},{20,24},{24,20},{28,32},{32,28},{36,40... | collective-permute-start | bytes 233480 | tf_op jit(solution)/shard_map/ppermute | solution.py:87
  12.4 3.7 %collective-permute-done.odd_ref = f32[19,8,128]{2,1,0:T(8,128)S(1)} collective-permute-done((f32[19,8,128]{2,1,0:T(8,128)S(1)}, f32[19,8,128]{2,1,0:T(8,128)S(1)}, u32[]{:S(2)}, u32[]{:S(2)}) %collective-permute-start) | collective-permute-done | bytes 77856 | tf_op jit(solution)/shard_map/ppermute | solution.py:87
  16.1 1.9 %collective-permute-start.2 = (f32[281,128]{1,0:T(8,128)S(1)}, f32[281,128]{1,0:T(8,128)S(1)}, u32[]{:S(2)}, u32[]{:S(2)}) collective-permute-start(f32[281,128]{1,0:T(8,128)S(1)} %get-tuple-element.42), channel_id=1, source_target_pairs={{1,2},{2,1},{5,6},{6,5},{9,10},{10,9},{13,14},{14,13},{17,18},{18,... | collective-permute-start | bytes 431624 | tf_op jit(solution)/shard_map/ppermute | solution.py:87
  18.1 0.1 collective-permute-start.3
  18.2 4.4 %collective-permute-done.2.odd_ref = f32[281,128]{1,0:T(8,128)S(1)} collective-permute-done((f32[281,128]{1,0:T(8,128)S(1)}, f32[281,128]{1,0:T(8,128)S(1)}, u32[]{:S(2)}, u32[]{:S(2)}) %collective-permute-start.2) | collective-permute-done | bytes 143904 | tf_op jit(solution)/shard_map/ppermute | solution.py:87
  22.6 3.2 %shard_map.61 = (f32[7,3,9,24,128]{4,3,2,1,0:T(8,128)S(1)}, f32[122,3,16,128]{3,2,1,0:T(8,128)S(1)}, f32[122,3,16,128]{3,2,1,0:T(8,128)S(1)}, f32[122,3,16,128]{...) custom-call(f32[2,19,8,128]{3,2,1,0:T(8,128)S(1)} %get-tuple-element, ...), custom_call_target="tpu_custom_call" | custom-call | tf_op jit(solution)/shard_map/pallas_call | solution.py:98
  25.8 7.7 %collective-permute-start.4 = (f32[64,128]{1,0:T(8,128)S(1)}, f32[64,128]{1,0:T(8,128)S(1)}, u32[]{:S(2)}, u32[]{:S(2)}) collective-permute-start(f32[64,128]{1,0:T(8,128)S(1)} %get-tuple-element.49), channel_id=1, source_target_pairs={{4,8},{8,4},{12,16},{16,12},{20,24},{24,20},{28,32},{32,28},{36,40... | collective-permute-start | bytes 98312 | tf_op jit(solution)/shard_map/ppermute | solution.py:87
  33.6 0.8 %shard_map.62.part_ref = f32[3,3,8,128]{3,2,1,0:T(8,128)S(1)} custom-call(f32[7,3,9,24,128]{4,3,2,1,0:T(8,128)S(1)} %get-tuple-element.44.rolled_ref, f32[122,3,16,128]{3,2,1,0:T(8,128)S(1)} %get-tuple-element.45.square_ref, f32[122,3,16,128]{3,2,1,0:T(8,128)S(1)} %get-tuple-element.46.along_ref, f32[122,3,16,128]{3,2,1,0:T(8,128)S(1)} %get-tuple-element.47.across_ref, ...), custom_call_target="tpu_custom_call" | custom-call | tf_op jit(solution)/shard_map/pallas_call | solution.py:98
  34.4 2.3 %collective-permute-done.4.odd_ref = f32[64,128]{1,0:T(8,128)S(1)} collective-permute-done((f32[64,128]{1,0:T(8,128)S(1)}, f32[64,128]{1,0:T(8,128)S(1)}, u32[]{:S(2)}, u32[]{:S(2)}) %collective-permute-start.4) | collective-permute-done | bytes 32800 | tf_op jit(solution)/shard_map/ppermute | solution.py:87
  36.7 0.8 %collective-permute-done.5.even_ref = f32[64,128]{1,0:T(8,128)S(1)} collective-permute-done((f32[64,128]{1,0:T(8,128)S(1)}, f32[64,128]{1,0:T(8,128)S(1)}, u32[]{:S(2)}, u32[]{:S(2)}) %collective-permute-start.5) | collective-permute-done | bytes 32800 | tf_op jit(solution)/shard_map/ppermute | solution.py:87
  37.5 0.6 shard_map.63
  38.1 1.9 %collective-permute-start.6 = (f32[54,128]{1,0:T(8,128)S(1)}, f32[54,128]{1,0:T(8,128)S(1)}, u32[]{:S(2)}, u32[]{:S(2)}) collective-permute-start(f32[54,128]{1,0:T(8,128)S(1)} %get-tuple-element.54), channel_id=1, source_target_pairs={{1,2},{2,1},{5,6},{6,5},{9,10},{10,9},{13,14},{14,13},{17,18},{18,... | collective-permute-start | bytes 82952 | tf_op jit(solution)/shard_map/ppermute | solution.py:87
  40.0 0.1 collective-permute-start.7
  40.1 3.2 %collective-permute-done.6.odd_ref = f32[54,128]{1,0:T(8,128)S(1)} collective-permute-done((f32[54,128]{1,0:T(8,128)S(1)}, f32[54,128]{1,0:T(8,128)S(1)}, u32[]{:S(2)}, u32[]{:S(2)}) %collective-permute-start.6) | collective-permute-done | bytes 27680 | tf_op jit(solution)/shard_map/ppermute | solution.py:87
  43.3 6.9 %collective-permute-start.8 = (f32[150,128]{1,0:T(8,128)S(1)}, f32[150,128]{1,0:T(8,128)S(1)}, u32[]{:S(2)}, u32[]{:S(2)}) collective-permute-start(f32[150,128]{1,0:T(8,128)S(1)} %get-tuple-element.56), channel_id=1, source_target_pairs={{4,8},{8,4},{12,16},{16,12},{20,24},{24,20},{28,32},{32,28},{36,40... | collective-permute-start | bytes 230408 | tf_op jit(solution)/shard_map/ppermute | solution.py:87
  50.3 1.4 %shard_map.65 = (f32[7,3,3,24,128]{4,3,2,1,0:T(8,128)S(1)}, f32[3,7,3,16,128]{4,3,2,1,0:T(8,128)S(1)}, f32[226,16,128]{2,1,0:T(8,128)S(1)}, f32[226,16,128]{2,1,...) custom-call(f32[3,3,24,128]{3,2,1,0:T(8,128)S(1)} %get-tuple-element.58.tall_ref, ...), custom_call_target="tpu_custom_call" | custom-call | tf_op jit(solution)/shard_map/pallas_call | solution.py:98
  51.8 3.5 %collective-permute-done.8.odd_ref = f32[150,128]{1,0:T(8,128)S(1)} collective-permute-done((f32[150,128]{1,0:T(8,128)S(1)}, f32[150,128]{1,0:T(8,128)S(1)}, u32[]{:S(2)}, u32[]{:S(2)}) %collective-permute-start.8) | collective-permute-done | bytes 76832 | tf_op jit(solution)/shard_map/ppermute | solution.py:87
  55.2 1.0 %shard_map.66 = (f32[7,3,6,24,128]{4,3,2,1,0:T(8,128)S(1)}, f32[140,16,128]{2,1,0:T(8,128)S(1)}, f32[140,16,128]{2,1,0:T(8,128)S(1)}, f32[140,16,128]{2,1,0:T(8,...) custom-call(f32[150,128]{1,0:T(8,128)S(1)} %collective-permute-done., ...), custom_call_target="tpu_custom_call" | custom-call | tf_op jit(solution)/shard_map/pallas_call | solution.py:98
  56.3 6.4 %collective-permute-start.10 = (f32[32,128]{1,0:T(8,128)S(1)}, f32[32,128]{1,0:T(8,128)S(1)}, u32[]{:S(2)}, u32[]{:S(2)}) collective-permute-start(f32[32,128]{1,0:T(8,128)S(1)} %get-tuple-element.62), channel_id=1, source_target_pairs={{4,8},{8,4},{12,16},{16,12},{20,24},{24,20},{28,32},{32,28},{36,40... | collective-permute-start | bytes 49160 | tf_op jit(solution)/shard_map/ppermute | solution.py:87
  62.7 0.8 %shard_map.67.part_ref = f32[3,3,8,128]{3,2,1,0:T(8,128)S(1)} custom-call(f32[7,3,3,24,128]{4,3,2,1,0:T(8,128)S(1)} %get-tuple-element.65.rolled_ref.inside_ref, f32[226,16,128]{2,1,0:T(8,128)S(1)} %get-tuple-element.70.square_ref, f32[226,16,128]{2,1,0:T(8,128)S(1)} %get-tuple-element.71.along_ref, f32[226,16,128]{2,1,0:T(8,128)S(1)} %get-tuple-element.72.across_ref, ...), custom_call_target="tpu_custom_call" | custom-call | tf_op jit(solution)/shard_map/pallas_call | solution.py:98
  63.5 3.5 %collective-permute-done.10.odd_ref = f32[32,128]{1,0:T(8,128)S(1)} collective-permute-done((f32[32,128]{1,0:T(8,128)S(1)}, f32[32,128]{1,0:T(8,128)S(1)}, u32[]{:S(2)}, u32[]{:S(2)}) %collective-permute-start.10) | collective-permute-done | bytes 16416 | tf_op jit(solution)/shard_map/ppermute | solution.py:87
  67.0 1.2 %shard_map.68 = (f32[3,3,8,128]{3,2,1,0:T(8,128)}, f32[3,8,128]{2,1,0:T(8,128)}) custom-call(f32[32,128]{1,0:T(8,128)S(1)} %collective-permute-done.10.odd_ref, f32[32,128]{1,0:T(8,128)S(1)} %collective-permute-done.11.even_ref, f32[7,3,6,24,128]{4,3,2,1,0:T(8,128)S(1)} %get-tuple-element.64.rolled_ref, ...), custom_call_target="tpu_custom_call" | custom-call | tf_op jit(solution)/shard_map/pallas_call | solution.py:98
  (10 shorter events, 0.4 us)
Async XLA Ops:
  1.5 10.9 %collective-permute-start.1 = (f32[19,8,128]{2,1,0:T(8,128)S(1)}, f32[19,8,128]{2,1,0:T(8,128)S(1)}, u32[]{:S(2)}, u32[]{:S(2)}) collective-permute-start(f32[19,8,128]{2,1,0:T(8,128)S(1)} %get-tuple-element.39.sent_ref), channel_id=1, source_target_pairs={{0,4},{4,0},{8,12},{12,8},{16,20},{20,16},{24,28},{28,24},{32,36},... | collective-permute-start | bytes 233480 | tf_op jit(solution)/shard_map/ppermute | solution.py:87
  3.2 12.9 %collective-permute-start = (f32[19,8,128]{2,1,0:T(8,128)S(1)}, f32[19,8,128]{2,1,0:T(8,128)S(1)}, u32[]{:S(2)}, u32[]{:S(2)}) collective-permute-start(f32[19,8,128]{2,1,0:T(8,128)S(1)} %get-tuple-element.39.sent_ref), channel_id=1, source_target_pairs={{4,8},{8,4},{12,16},{16,12},{20,24},{24,20},{28,32},{32,28},{36,40... | collective-permute-start | bytes 233480 | tf_op jit(solution)/shard_map/ppermute | solution.py:87
  16.1 6.5 %collective-permute-start.2 = (f32[281,128]{1,0:T(8,128)S(1)}, f32[281,128]{1,0:T(8,128)S(1)}, u32[]{:S(2)}, u32[]{:S(2)}) collective-permute-start(f32[281,128]{1,0:T(8,128)S(1)} %get-tuple-element.42), channel_id=1, source_target_pairs={{1,2},{2,1},{5,6},{6,5},{9,10},{10,9},{13,14},{14,13},{17,18},{18,... | collective-permute-start | bytes 431624 | tf_op jit(solution)/shard_map/ppermute | solution.py:87
  18.1 4.5 %collective-permute-start.3 = (f32[281,128]{1,0:T(8,128)S(1)}, f32[281,128]{1,0:T(8,128)S(1)}, u32[]{:S(2)}, u32[]{:S(2)}) collective-permute-start(f32[281,128]{1,0:T(8,128)S(1)} %get-tuple-element.43), channel_id=1, source_target_pairs={{0,1},{1,0},{2,3},{3,2},{4,5},{5,4},{6,7},{7,6},{8,9},{9,8},{10,11... | collective-permute-start | bytes 431624 | tf_op jit(solution)/shard_map/ppermute | solution.py:87
  25.8 10.9 %collective-permute-start.4 = (f32[64,128]{1,0:T(8,128)S(1)}, f32[64,128]{1,0:T(8,128)S(1)}, u32[]{:S(2)}, u32[]{:S(2)}) collective-permute-start(f32[64,128]{1,0:T(8,128)S(1)} %get-tuple-element.49), channel_id=1, source_target_pairs={{4,8},{8,4},{12,16},{16,12},{20,24},{24,20},{28,32},{32,28},{36,40... | collective-permute-start | bytes 98312 | tf_op jit(solution)/shard_map/ppermute | solution.py:87
  33.5 4.0 %collective-permute-start.5 = (f32[64,128]{1,0:T(8,128)S(1)}, f32[64,128]{1,0:T(8,128)S(1)}, u32[]{:S(2)}, u32[]{:S(2)}) collective-permute-start(f32[64,128]{1,0:T(8,128)S(1)} %get-tuple-element.50), channel_id=1, source_target_pairs={{0,4},{4,0},{8,12},{12,8},{16,20},{20,16},{24,28},{28,24},{32,36},... | collective-permute-start | bytes 98312 | tf_op jit(solution)/shard_map/ppermute | solution.py:87
  38.1 5.2 %collective-permute-start.6 = (f32[54,128]{1,0:T(8,128)S(1)}, f32[54,128]{1,0:T(8,128)S(1)}, u32[]{:S(2)}, u32[]{:S(2)}) collective-permute-start(f32[54,128]{1,0:T(8,128)S(1)} %get-tuple-element.54), channel_id=1, source_target_pairs={{1,2},{2,1},{5,6},{6,5},{9,10},{10,9},{13,14},{14,13},{17,18},{18,... | collective-permute-start | bytes 82952 | tf_op jit(solution)/shard_map/ppermute | solution.py:87
  40.0 3.3 %collective-permute-start.7 = (f32[54,128]{1,0:T(8,128)S(1)}, f32[54,128]{1,0:T(8,128)S(1)}, u32[]{:S(2)}, u32[]{:S(2)}) collective-permute-start(f32[54,128]{1,0:T(8,128)S(1)} %get-tuple-element.55), channel_id=1, source_target_pairs={{0,1},{1,0},{2,3},{3,2},{4,5},{5,4},{6,7},{7,6},{8,9},{9,8},{10,11... | collective-permute-start | bytes 82952 | tf_op jit(solution)/shard_map/ppermute | solution.py:87
  43.3 12.0 %collective-permute-start.8 = (f32[150,128]{1,0:T(8,128)S(1)}, f32[150,128]{1,0:T(8,128)S(1)}, u32[]{:S(2)}, u32[]{:S(2)}) collective-permute-start(f32[150,128]{1,0:T(8,128)S(1)} %get-tuple-element.56), channel_id=1, source_target_pairs={{4,8},{8,4},{12,16},{16,12},{20,24},{24,20},{28,32},{32,28},{36,40... | collective-permute-start | bytes 230408 | tf_op jit(solution)/shard_map/ppermute | solution.py:87
  50.2 5.0 %collective-permute-start.9 = (f32[150,128]{1,0:T(8,128)S(1)}, f32[150,128]{1,0:T(8,128)S(1)}, u32[]{:S(2)}, u32[]{:S(2)}) collective-permute-start(f32[150,128]{1,0:T(8,128)S(1)} %get-tuple-element.57), channel_id=1, source_target_pairs={{0,4},{4,0},{8,12},{12,8},{16,20},{20,16},{24,28},{28,24},{32,36},... | collective-permute-start | bytes 230408 | tf_op jit(solution)/shard_map/ppermute | solution.py:87
  56.3 10.7 %collective-permute-start.10 = (f32[32,128]{1,0:T(8,128)S(1)}, f32[32,128]{1,0:T(8,128)S(1)}, u32[]{:S(2)}, u32[]{:S(2)}) collective-permute-start(f32[32,128]{1,0:T(8,128)S(1)} %get-tuple-element.62), channel_id=1, source_target_pairs={{4,8},{8,4},{12,16},{16,12},{20,24},{24,20},{28,32},{32,28},{36,40... | collective-permute-start | bytes 49160 | tf_op jit(solution)/shard_map/ppermute | solution.py:87
  62.6 4.4 %collective-permute-start.11 = (f32[32,128]{1,0:T(8,128)S(1)}, f32[32,128]{1,0:T(8,128)S(1)}, u32[]{:S(2)}, u32[]{:S(2)}) collective-permute-start(f32[32,128]{1,0:T(8,128)S(1)} %get-tuple-element.63), channel_id=1, source_target_pairs={{0,4},{4,0},{8,12},{12,8},{16,20},{20,16},{24,28},{28,24},{32,36},... | collective-permute-start | bytes 49160 | tf_op jit(solution)/shard_map/ppermute | solution.py:87
